TPU v7x, 32 devices: a whole 2x2x4 slice. The times are simulated.
32 devices in a mesh: run: 2 (over y), gx: 4 (over x, core), gy: 4 (over z).
Axes of the slice: x: 2, y: 2, z: 4, core: 2. Of those that a mesh axis runs over, the one named last changes fastest.
Arguments:
- magnet: float32 [3, 4, 256, 256], P(None, None, ('run', 'gx', 'gy')), parts along dimension 2, may hold values from -1 to 1, as said below
- window_shift: int32 [2], P('run'), parts along dimension 0, may hold values from 1 to 7
- region: int32 [256, 256], P(('run', 'gx', 'gy')), parts along dimension 0, may hold values 0 or 1
- material: float32 [4, 5], replicated, may hold values from 0.1 to 1
- kernel: float32 [6, 7, 256, 256], P(None, None, ('gx', 'gy')), may hold values from -6 to 6, as said below
Outputs:
- magnet_next: float32 [3, 4, 256, 256], P(None, None, ('run', 'gx', 'gy')), parts along dimension 2
- effective_field: float32 [3, 4, 256, 256], P(None, None, ('run', 'gx', 'gy')), parts along dimension 2
There are 2 independent parts, one for each index of `run`. A program takes and returns all parts, laid end to end along the dimension named above; an argument that names none is the same for every part. Nothing has to cross between parts.
Inputs may be any that keep to these rules, and one draw needn't show every extreme that they name: `magnet`: each cell's three components form a unit vector. kernel[c, d, ky, kx] equals t_c kernel[c, d, ky, (256 - kx) mod 256] with t_c = -1 for c = 3 and 4, 1 otherwise; it equals u_c kernel[c, 6 - d, ky, kx] with u_c = -1 for c = 4 and 5, 1 otherwise; components 3 and 5 are zero at ky = 0.
All inputs are finite; a program needn't handle non-finite values. No bound on the sum of `region` on one device may be relied on, other than what follows from the above.
Results may differ from a plain program's by a relative error of at most 0.0001.
Values sent between devices are 32-bit elements; how exact they have to be, the bound alone decides.
No kernel may reach another device: no remote copies, remote signals or barrier semaphores. Data moves between devices by JAX's collectives and lax.ppermute only.
A program may use at most 128 MiB of HBM per device.

v0:
```python
import functools
import math

import jax
import jax.numpy as jnp
import numpy as np
from jax import lax
from jax.experimental import pallas as pl
from jax.experimental.pallas import tpu as pltpu
from jax.sharding import PartitionSpec as P

time_step = 0.1
pair_comp = ((0, 3, 4), (3, 1, 5), (4, 5, 2))
highest = lax.Precision.HIGHEST
lanes = 128


def passed_along(value, axis, steps):
    count = lax.axis_size(axis)
    leading, last = (max(0, -steps), min(count, count - steps))
    return lax.ppermute(value, axis, [(source, source + steps) for source in range(leading, last)])


def with_halo(cells, sides, width):
    for axis, dim in sides:
        count = lax.axis_size(axis)
        ends = count - 1
        head = lax.slice_in_dim(cells, 0, width, axis=dim)
        tail = lax.slice_in_dim(cells, cells.shape[dim] - width, cells.shape[dim], axis=dim)
        cells = jnp.concatenate(
            [
                lax.ppermute(tail, axis, [(i, (i + 1) % count) for i in range(ends)]),
                cells,
                lax.ppermute(head, axis, [((i + 1) % count, i) for i in range(ends)]),
            ],
            axis=dim,
        )
    return cells


def cross_product(left, right):
    return jnp.stack(
        [
            left[1] * right[2] - left[2] * right[1],
            left[2] * right[0] - left[0] * right[2],
            left[0] * right[1] - left[1] * right[0],
        ]
    )


def phases(count_rows, count_cols, length, direction):
    product = (
        jnp.arange(count_rows, dtype=jnp.int32)[:, None]
        * jnp.arange(count_cols, dtype=jnp.int32)[None, :]
        % length
    )
    angles = direction * 2.0 * math.pi / length * product.astype(jnp.float32)
    return (jnp.cos(angles), jnp.sin(angles))


def complex_table(cosine, sine):
    top_rows = jnp.stack([cosine, sine], axis=1)
    bottom_rows = jnp.stack([-sine, cosine], axis=1)
    return jnp.stack([top_rows, bottom_rows], axis=0)


def twist(first_pass, cosine, sine):
    real_part = first_pass[:, 0]
    imag_part = first_pass[:, 1]
    return jnp.stack(
        [real_part * cosine - imag_part * sine, real_part * sine + imag_part * cosine], axis=1
    )


def forward_track(values):
    batch, pair, track_cells = values.shape
    track_freq = 2 * track_cells
    outer_len = track_freq // 64
    outer_used = track_cells // 64
    blocked = values.reshape(batch, 2, outer_used, 64)
    cosine, sine = phases(outer_used, outer_len, outer_len, -1.0)
    first_pass = jnp.einsum(
        "bpxa,pxqk->bqka", blocked, complex_table(cosine, sine), precision=highest
    )
    twist_cos, twist_sin = phases(outer_len, 64, track_freq, -1.0)
    twisted = twist(first_pass, twist_cos, twist_sin)
    cosine, sine = phases(64, 64, 64, -1.0)
    result = jnp.einsum("bpka,paqj->bqjk", twisted, complex_table(cosine, sine), precision=highest)
    return result.reshape(batch, 2, track_freq)


def inverse_track(values):
    batch, pair, track_freq = values.shape
    track_cells = track_freq // 2
    outer_len = track_freq // 64
    outer_used = track_cells // 64
    blocked = values.reshape(batch, 2, 64, outer_len)
    cosine, sine = phases(64, 64, 64, 1.0)
    first_pass = jnp.einsum(
        "bpjk,pjqa->bqka", blocked, complex_table(cosine, sine), precision=highest
    )
    twist_cos, twist_sin = phases(outer_len, 64, track_freq, 1.0)
    twisted = twist(first_pass, twist_cos, twist_sin)
    cosine, sine = phases(outer_len, outer_used, outer_len, 1.0)
    result = jnp.einsum("bpka,pkqx->bqxa", twisted, complex_table(cosine, sine), precision=highest)
    return result.reshape(batch, 2, track_cells)


def apply_kernel(spectrum, kernel_pairs):
    fields = []
    for i in range(3):
        summed = None
        for j in range(3):
            index_c = pair_comp[i][j]
            table = kernel_pairs[index_c][:, :, :, None, :]
            contrib = jnp.sum(table * spectrum[j][None], axis=1)
            if index_c >= 4:
                contrib = jnp.stack([-contrib[:, :, 1], contrib[:, :, 0]], axis=2)
            summed = contrib if summed is None else summed + contrib
        fields.append(summed)
    return jnp.stack(fields)


def clamp_ends(widened, position, devices):
    head_row = jnp.where(position == 0, widened[:, :, 1:2], widened[:, :, 0:1])
    tail_row = jnp.where(position == devices - 1, widened[:, :, -2:-1], widened[:, :, -1:])
    return jnp.concatenate([head_row, widened[:, :, 1:-1], tail_row], axis=2)


def demag_field(state, kernel_pairs, forward_y, inverse_y):
    components, layers, slab_rows, width_cells = state.shape
    devices = lax.axis_size(("gx", "gy"))
    local_freq = width_cells // devices
    track_cells = slab_rows * devices
    track_freq = 2 * track_cells
    spectrum = jnp.einsum("czxy,ypk->czkpx", state, forward_y, precision=highest)
    blocks = spectrum.reshape(components, layers, devices, local_freq, 2, 1, slab_rows)
    arrived = lax.all_to_all(blocks, ("gx", "gy"), split_axis=2, concat_axis=5, tiled=True)
    flat_rows = arrived.reshape(components * layers * local_freq, 2, track_cells)
    spectrum_x = forward_track(flat_rows).reshape(components, layers, local_freq, 2, track_freq)
    product_hat = apply_kernel(spectrum_x, kernel_pairs)
    returned_x = inverse_track(product_hat.reshape(components * layers * local_freq, 2, track_freq))
    pieces = returned_x.reshape(components, layers, 1, local_freq, 2, devices, slab_rows)
    landed = lax.all_to_all(pieces, ("gx", "gy"), split_axis=5, concat_axis=2, tiled=True)
    gathered_y = landed.reshape(components, layers, width_cells, 2, slab_rows)
    return jnp.einsum("czkpx,kpy->czxy", gathered_y, inverse_y, precision=highest)


def local(magnet, window_shift, region, material, kernel):
    components, layers, slab_rows, width_cells = magnet.shape
    devices = lax.axis_size(("gx", "gy"))
    position = lax.axis_index(("gx", "gy"))
    track_cells = slab_rows * devices
    track_freq = 2 * track_cells
    freq_len = 2 * width_cells - 1
    offset = window_shift[0]
    fill_up = (jnp.arange(3) == 2).astype(jnp.float32).reshape(3, 1, 1, 1)
    following = passed_along(magnet, ("gx", "gy"), -1)
    joined = jnp.concatenate([magnet, following], axis=2)
    widened = lax.dynamic_slice_in_dim(joined, offset - 1, slab_rows + 2, 2)
    global_cell = position * slab_rows - 1 + jnp.arange(slab_rows + 2, dtype=jnp.int32)
    widened = jnp.where(
        (global_cell >= track_cells - offset)[None, None, :, None], fill_up, widened
    )
    initial = widened[:, :, 1:-1]
    first_widened = clamp_ends(widened, position, devices)
    dz_table = np.arange(layers)[:, None] - np.arange(layers)[None, :] + layers - 1
    kernel_pairs = kernel[:, dz_table]
    cosine, sine = phases(width_cells, width_cells, freq_len, -1.0)
    forward_y = jnp.stack([cosine, sine], axis=1)
    cosine, sine = phases(width_cells, width_cells, freq_len, 1.0)
    weight = jnp.where(jnp.arange(width_cells) == 0, 1.0, 2.0).astype(jnp.float32)[:, None]
    inverse_y = jnp.stack([weight * cosine, -weight * sine], axis=1) / float(track_freq * freq_len)
    damping = material[:, 0].reshape(1, layers, 1, 1)
    nonadiabatic = material[:, 1].reshape(1, layers, 1, 1)
    stiffness = material[:, 2].reshape(1, layers, 1, 1)
    anisotropy = material[:, 3].reshape(1, layers, 1, 1)
    drift_speed = material[:, 4].reshape(1, layers, 1, 1) * region.astype(jnp.float32)[None, None]

    def rate_of(state, widened_in):
        if widened_in is None:
            widened_in = clamp_ends(with_halo(state, ((("gx", "gy"), 2),), 1), position, devices)
        width_pad = jnp.pad(state, ((0, 0), (0, 0), (0, 0), (1, 1)), mode="edge")
        layer_pad = jnp.pad(state, ((0, 0), (1, 1), (0, 0), (0, 0)), mode="edge")
        laplace = widened_in[:, :, 2:] + widened_in[:, :, :-2]
        laplace = laplace + width_pad[:, :, :, 2:] + width_pad[:, :, :, :-2]
        laplace = laplace + layer_pad[:, 2:] + layer_pad[:, :-2] - 6.0 * state
        slope = 0.5 * (widened_in[:, :, 2:] - widened_in[:, :, :-2])
        effective = stiffness * laplace + anisotropy * state[2:3] * fill_up
        effective = effective + demag_field(state, kernel_pairs, forward_y, inverse_y)
        drift_term = drift_speed * slope
        torque_h = cross_product(state, effective)
        damping_h = cross_product(state, torque_h)
        torque_u = cross_product(state, drift_term)
        damping_u = cross_product(state, torque_u)
        change = (
            -torque_h
            - damping * damping_h
            + (1.0 + damping * nonadiabatic) * damping_u
            + (nonadiabatic - damping) * torque_u
        ) / (1.0 + damping * damping)
        return (change, effective)

    section_one, effective_field = rate_of(initial, first_widened)
    section_two, _ = rate_of(initial + 0.5 * time_step * section_one, None)
    section_three, _ = rate_of(initial + 0.5 * time_step * section_two, None)
    section_four, _ = rate_of(initial + time_step * section_three, None)
    magnet_next = initial + time_step / 6.0 * (
        section_one + 2.0 * section_two + 2.0 * section_three + section_four
    )
    return (magnet_next, effective_field)


def split_table(table):
    table = np.asarray(table, np.float64).astype(np.float32)
    high = table.astype(jnp.bfloat16)
    low = (table - high.astype(np.float32)).astype(jnp.bfloat16)
    return (high, low)


def angle_table(rows, cols, length):
    product = np.outer(np.arange(rows), np.arange(cols)) % length
    return 2.0 * np.pi / length * product


def width_tables(width_cells, devices, scale):
    freq_len = 2 * width_cells - 1
    angles = angle_table(width_cells, width_cells, freq_len)
    shape = (width_cells, devices, 1, width_cells // devices)
    cosine, sine = np.cos(angles).reshape(shape), np.sin(angles).reshape(shape)
    forward = np.concatenate([cosine, -sine], axis=2).reshape(width_cells, 2 * width_cells)
    weight = np.where(np.arange(width_cells) == 0, 1.0, 2.0).reshape(shape[1:]) * scale
    inverse = np.concatenate([weight * cosine, -weight * sine], axis=2)
    return (forward, inverse.reshape(width_cells, 2 * width_cells).T)


def track_tables(track_cells):
    angles = angle_table(track_cells, track_cells, 2 * track_cells)
    cosine, sine = np.cos(angles), np.sin(angles)
    sine[:, 0] = np.where(np.arange(track_cells) % 2 == 0, 1.0, -1.0)
    weight = np.where(np.arange(track_cells) == 0, 1.0, 2.0)
    forward = np.concatenate([cosine, sine], axis=1)
    inverse = np.concatenate([weight * cosine, weight * sine], axis=1)
    return (forward, inverse)


def halves(value):
    high = value.astype(jnp.bfloat16)
    return (high, (value - high.astype(jnp.float32)).astype(jnp.bfloat16))


def dot_halves(left, right, dims=((1,), (0,))):
    def dot(a, b):
        return lax.dot_general(a, b, (dims, ((), ())), preferred_element_type=jnp.float32)

    return dot(left[0], right[0]) + (dot(left[0], right[1]) + dot(left[1], right[0]))


def turn_blocks(blocks, size):
    count = len(blocks)
    group = lax.broadcasted_iota(jnp.int32, blocks[0].shape, 1) // size
    results = []
    for j in range(count):
        result = None
        for i in range(count):
            shift = (i - j) * size % (count * size)
            moved = pltpu.roll(blocks[i], shift, 1) if shift else blocks[i]
            result = moved if result is None else jnp.where(group == i, moved, result)
        results.append(result)
    return results


def send_forward(cells, forward_refs, send_ref, devices):
    slab_rows = send_ref.shape[1]
    size = 2 * forward_refs[0].shape[0] // devices
    per_tile = lanes // size
    spectrum = dot_halves(halves(cells), (forward_refs[0][...], forward_refs[1][...]))
    fields = cells.shape[0] // slab_rows
    for a in range(fields // per_tile):
        for q in range(devices // per_tile):
            blocks = [
                spectrum[(a * per_tile + b) * slab_rows : (a * per_tile + b + 1) * slab_rows, q * lanes : (q + 1) * lanes]
                for b in range(per_tile)
            ]
            for b, block in enumerate(turn_blocks(blocks, size)):
                send_ref[q * per_tile + b, :, a * lanes : (a + 1) * lanes] = block


def take_inverse(received_ref, inverse_refs, rows_ref):
    devices, slab_rows, width = received_ref.shape
    size = inverse_refs[0].shape[0] // devices
    per_tile = lanes // size
    fields = width // size
    for a in range(fields // per_tile):
        for q in range(devices // per_tile):
            blocks = [
                received_ref[q * per_tile + b, :, a * lanes : (a + 1) * lanes] for b in range(per_tile)
            ]
            for b, block in enumerate(turn_blocks(blocks, size)):
                row = (a * per_tile + b) * slab_rows
                rows_ref[row : row + slab_rows, q * lanes : (q + 1) * lanes] = block
    return dot_halves(halves(rows_ref[...]), (inverse_refs[0][...], inverse_refs[1][...]))


def window_kernel(devices, place_ref, magnet_ref, following_ref, *refs):
    forward_refs = refs[:2]
    initial_ref, before_ref, after_ref, send_ref, joined_ref, moved_ref = refs[2:]
    components, layers, slab_rows, width = magnet_ref.shape
    fields = components * layers
    position = place_ref[0]
    offset = place_ref[1]
    limit = devices * slab_rows - offset - position * slab_rows
    joined_ref[:, 0:slab_rows, :] = magnet_ref[...].reshape(fields, slab_rows, width)
    joined_ref[:, slab_rows : 2 * slab_rows, :] = following_ref[...].reshape(fields, slab_rows, width)

    for choice in range(1, slab_rows):

        @pl.when(offset == choice)
        def move():
            for f in range(fields):
                moved_ref[f] = joined_ref[f, choice : choice + slab_rows, :]
                before_ref[f : f + 1, :] = joined_ref[f, choice - 1 : choice, :]
                after_ref[f : f + 1, :] = joined_ref[f, choice + slab_rows : choice + slab_rows + 1, :]

    def filled(rows, cell, field):
        return jnp.where(cell >= limit, jnp.where(field >= fields - layers, 1.0, 0.0), rows)

    rows = moved_ref[...]
    cell = lax.broadcasted_iota(jnp.int32, rows.shape, 1)
    state = filled(rows, cell, lax.broadcasted_iota(jnp.int32, rows.shape, 0))
    edge = lax.broadcasted_iota(jnp.int32, (fields, width), 0)
    before_ref[...] = filled(before_ref[...], jnp.full((fields, width), -1, jnp.int32), edge)
    after_ref[...] = filled(after_ref[...], jnp.full((fields, width), slab_rows, jnp.int32), edge)
    initial_ref[...] = state.reshape(components, layers, slab_rows, width)
    send_forward(state.reshape(fields * slab_rows, width), forward_refs, send_ref, devices)


def track_kernel(received_ref, table_ref, wf_high, wf_low, wi_high, wi_low, send_ref, spectrum_ref, product_ref):
    devices, slab_rows, width = received_ref.shape
    components = 3
    layers, local_freq = table_ref.shape[1:3]
    track = devices * slab_rows
    flat = received_ref[...].reshape(track, width).T
    spectrum_ref[...] = dot_halves(halves(flat), (wf_high[...], wf_low[...]))
    step = 8
    first_lane = lax.broadcasted_iota(jnp.int32, (step, track), 1) == 0
    for start in range(0, local_freq, step):

        def part(j, w, p, half):
            row = ((j * layers + w) * 2 + p) * local_freq + start
            return (slice(row, row + step), slice(half * track, (half + 1) * track))

        tables = {}
        for c in range(6):
            for e in range(layers):
                cosine = table_ref[c, e, start : start + step, 0:track]
                nyquist = table_ref[c, e, start : start + step, track : 2 * track]
                tables[c, e] = (cosine, jnp.where(first_lane, nyquist, cosine) if c in (0, 1, 2, 5) else cosine)
        for i in range(components):
            for z in range(layers):
                sums = [None] * 4

                def add(slot, value, sign):
                    if sums[slot] is None:
                        sums[slot] = value if sign > 0 else -value
                    else:
                        sums[slot] = sums[slot] + value if sign > 0 else sums[slot] - value

                for j in range(components):
                    c = pair_comp[i][j]
                    for w in range(layers):
                        even, odd = tables[c, abs(z - w)]
                        sign = -1 if z < w and c >= 4 else 1
                        ac, as_, bc, bs = [
                            spectrum_ref[part(j, w, p, half)] for p in range(2) for half in range(2)
                        ]
                        if c <= 2:
                            terms = ((even * ac, 1), (odd * as_, 1), (even * bc, 1), (odd * bs, 1))
                        elif c == 3:
                            terms = ((even * bs, 1), (even * bc, -1), (even * as_, -1), (even * ac, 1))
                        elif c == 4:
                            terms = ((even * as_, 1), (even * ac, -1), (even * bs, 1), (even * bc, -1))
                        else:
                            terms = ((even * bc, -1), (odd * bs, -1), (even * ac, 1), (odd * as_, 1))
                        for slot, (value, term_sign) in enumerate(terms):
                            add(slot, value, term_sign * sign)
                for slot in range(4):
                    product_ref[part(i, z, slot // 2, slot % 2)] = sums[slot]
    result = dot_halves((wi_high[...], wi_low[...]), halves(product_ref[...]), ((1,), (1,)))
    send_ref[...] = result.reshape(devices, slab_rows, width)


def step_kernel(stage, devices, place_ref, coef_ref, received_ref, state_ref, before_ref, after_ref, region_ref, *refs):
    refs = list(refs)
    inverse_refs = [refs.pop(0), refs.pop(0)]
    forward_refs = [refs.pop(0), refs.pop(0)] if stage < 3 else None
    initial_ref = refs.pop(0) if stage > 0 else state_ref
    sum_ref = refs.pop(0) if stage > 0 else None
    field_ref = refs.pop(0) if stage == 0 else None
    next_ref = refs.pop(0)
    if stage < 3:
        total_ref, head_ref, tail_ref, send_ref = [refs.pop(0) for _ in range(4)]
    rows_ref = refs.pop(0)
    components, layers, slab_rows, width = state_ref.shape
    position = place_ref[0]
    demag = take_inverse(received_ref, inverse_refs, rows_ref)
    shape = (slab_rows, width)
    row = lax.broadcasted_iota(jnp.int32, shape, 0)
    col = lax.broadcasted_iota(jnp.int32, shape, 1)
    flow = region_ref[...].astype(jnp.float32)
    is_first = (position == 0).astype(jnp.int32)
    is_last = (position == devices - 1).astype(jnp.int32)
    fields = []
    moved = []
    for z in range(layers):
        stiffness, anisotropy, drift = (coef_ref[z, 4], coef_ref[z, 5], coef_ref[z, 6])
        m, h, g = ([], [], [])
        for c in range(components):
            f = c * layers + z
            cells = state_ref[c, z]
            head = jnp.where(is_first == 1, cells[0:1], before_ref[f : f + 1, :])
            tail = jnp.where(is_last == 1, cells[slab_rows - 1 : slab_rows], after_ref[f : f + 1, :])
            lower = jnp.where(row == 0, head, pltpu.roll(cells, 1, 0))
            upper = jnp.where(row == slab_rows - 1, tail, pltpu.roll(cells, slab_rows - 1, 0))
            left = jnp.where(col == 0, cells, pltpu.roll(cells, 1, 1))
            right = jnp.where(col == width - 1, cells, pltpu.roll(cells, width - 1, 1))
            laplace = (upper + lower) + (left + right)
            laplace = laplace + state_ref[c, max(z - 1, 0)] + state_ref[c, min(z + 1, layers - 1)] - 6.0 * cells
            effective = stiffness * laplace + demag[f * slab_rows : (f + 1) * slab_rows, :]
            if c == 2:
                effective = effective + anisotropy * cells
            if stage == 0:
                field_ref[c, z] = effective
            m.append(cells)
            h.append(effective)
            g.append((0.5 * drift) * flow * (upper - lower))
        inner = [coef_ref[z, 1] * h[c] + coef_ref[z, 2] * g[c] for c in range(3)]
        outer = [coef_ref[z, 0] * h[c] + coef_ref[z, 3] * g[c] for c in range(3)]
        turned = [m[(c + 1) % 3] * inner[(c + 2) % 3] - m[(c + 2) % 3] * inner[(c + 1) % 3] for c in range(3)]
        whole = [outer[c] + turned[c] for c in range(3)]
        for c in range(components):
            rate = m[(c + 1) % 3] * whole[(c + 2) % 3] - m[(c + 2) % 3] * whole[(c + 1) % 3]
            start = initial_ref[c, z]
            if stage == 3:
                next_ref[c, z] = start + (time_step / 6.0) * (sum_ref[c, z] + rate)
            else:
                factor = time_step if stage == 2 else 0.5 * time_step
                value = start + factor * rate
                next_ref[c, z] = value
                f = c * layers + z
                head_ref[f : f + 1, :] = value[0:1]
                tail_ref[f : f + 1, :] = value[slab_rows - 1 : slab_rows]
                total_ref[c, z] = rate if stage == 0 else sum_ref[c, z] + 2.0 * rate
    if stage < 3:
        cells = next_ref[...].reshape(components * layers * slab_rows, width)
        send_forward(cells, forward_refs, send_ref, devices)


def call(body, name, outs, in_smem, args, scratch):
    in_specs = [
        pl.BlockSpec(memory_space=pltpu.SMEM if i < in_smem else pltpu.VMEM) for i in range(len(args))
    ]
    return pl.pallas_call(
        body,
        name=name,
        out_shape=[jax.ShapeDtypeStruct(s, jnp.float32) for s in outs],
        in_specs=in_specs,
        out_specs=[pl.BlockSpec(memory_space=pltpu.VMEM) for _ in outs],
        scratch_shapes=[pltpu.VMEM(s, jnp.float32) for s in scratch],
        compiler_params=pltpu.CompilerParams(vmem_limit_bytes=24 * 1024 * 1024),
    )(*args)


def exchange(blocks):
    return lax.all_to_all(blocks, ("gx", "gy"), split_axis=0, concat_axis=0, tiled=True)


def local_tiled(magnet, window_shift, region, material, kernel):
    components, layers, slab_rows, width = magnet.shape
    devices = lax.axis_size(("gx", "gy"))
    position = lax.axis_index(("gx", "gy"))
    track = slab_rows * devices
    fields = components * layers
    scale = 1.0 / (2 * track * (2 * width - 1))
    forward, inverse = [split_table(t) for t in width_tables(width, devices, scale)]
    track_forward, track_inverse = [split_table(t) for t in track_tables(track)]
    row_width = 2 * fields * (width // devices)
    block_shape = (devices, slab_rows, row_width)
    following = passed_along(magnet, ("gx", "gy"), -1)
    place = jnp.stack([position.astype(jnp.int32), window_shift[0]])
    a, b = (material[:, 0], material[:, 1])
    below = 1.0 / (1.0 + a * a)
    zero = jnp.zeros_like(a)
    coef = jnp.stack(
        [-below, -a * below, (1.0 + a * b) * below, (b - a) * below, material[:, 2], material[:, 3], material[:, 4], zero],
        axis=1,
    )
    table = kernel[:, layers - 1 :]
    initial, before, after, send = call(
        functools.partial(window_kernel, devices),
        "window",
        [magnet.shape, (fields, width), (fields, width), block_shape],
        1,
        [place, magnet, following, *forward],
        [(fields, 2 * slab_rows, width), (fields, slab_rows, width)],
    )
    state = initial
    total = None
    for stage in range(4):
        received = exchange(send)
        (back,) = call(
            track_kernel,
            "track",
            [block_shape],
            0,
            [received, table, *track_forward, *track_inverse],
            [(row_width, 2 * track), (row_width, 2 * track)],
        )
        returned = exchange(back)
        args = [place, coef, returned, state, before, after, region, *inverse]
        outs = [magnet.shape]
        if stage < 3:
            args += [*forward]
            outs += [magnet.shape, (fields, width), (fields, width), block_shape]
        if stage > 0:
            args += [initial, total]
        else:
            outs = [magnet.shape] + outs
        results = list(
            call(
                functools.partial(step_kernel, stage, devices),
                "step",
                outs,
                2,
                args,
                [(fields * slab_rows, 2 * width)],
            )
        )
        if stage == 0:
            effective_field = results.pop(0)
        state = results.pop(0)
        if stage < 3:
            total, head, tail, send = results
            before = passed_along(tail, ("gx", "gy"), 1)
            after = passed_along(head, ("gx", "gy"), -1)
    return (state, effective_field)


def fits_tiles(mesh_devices, width):
    size = 2 * (width // mesh_devices)
    return size % 16 == 0 and lanes % size == 0 and mesh_devices % (lanes // size) == 0


def local_any(magnet, window_shift, region, material, kernel):
    components, layers, slab_rows, width = magnet.shape
    devices = lax.axis_size(("gx", "gy"))
    track = slab_rows * devices
    per_tile = lanes * devices // (2 * width)
    tiled = fits_tiles(devices, width) and slab_rows % 8 == 0 and track % lanes == 0 and width % lanes == 0
    tiled = tiled and components * layers % max(per_tile, 1) == 0
    return (local_tiled if tiled else local)(magnet, window_shift, region, material, kernel)


def solution(mesh):
    in_specs = (
        P(None, None, ("run", "gx", "gy"), None),
        P("run"),
        P(("run", "gx", "gy"), None),
        P(),
        P(None, None, ("gx", "gy"), None),
    )
    out_specs = (P(None, None, ("run", "gx", "gy"), None), P(None, None, ("run", "gx", "gy"), None))
    return jax.shard_map(local_any, mesh=mesh, in_specs=in_specs, out_specs=out_specs, check_vma=False)
```

profile of v0, /device:TPU:0, one launch (start us, length us, event | category | flops | bytes accessed | tf_op | source)
XLA Modules:
  0.0 136.0 jit_solution(1357294607577089711)
XLA Ops:
  0.6 1.3 collective-permute-start
  2.6 0.1 pad_add_fusion.place_ref
  2.7 5.9 %collective-permute-done.following_ref = f32[3,4,8,256]{3,2,1,0:T(8,128)S(1)} collective-permute-done((f32[3,4,8,256]{3,2,1,0:T(8,128)}, f32[3,4,8,256]{3,2,1,0:T(8,128)S(1)}, u32[]{:S(2)}, u32[]{:S(2)}) %collective-permute-start) | collective-permute-done | bytes 98336 | tf_op jit(solution)/shard_map/ppermute | solution.py:21
  8.6 0.0 copy-start
  8.6 0.9 copy-done
  9.5 0.0 copy-start.2
  9.5 0.9 copy-done.2
  10.5 0.0 copy-start.11
  10.5 0.9 copy-done.11
  11.4 1.7 %window.1 = (f32[3,4,8,256]{3,2,1,0:T(8,128)S(1)}, f32[12,256]{1,0:T(8,128)S(1)}, f32[12,256]{1,0:T(8,128)S(1)}, f32[16,8,384]{2,1,0:T(8,128)}) custom-call(s32[2]{0:T(128)S(1)} %pad_add_fusion.place_ref, f32[3,4,8,256]{3,2,1,0:T(8,128)S(1)} %copy-done.11, f32[3,4,8,256]{3,2,1,0:T(8,128)S(1)} %collective-permute-done.following_ref, ...), custom_call_target="tpu_custom_call" | custom-call | tf_op jit(solution)/shard_map/window/pallas_call | solution.py:463
  13.1 8.4 %all-to-all-start = ((f32[16,8,384]{2,1,0:T(8,128)}), f32[16,8,384]{2,1,0:T(8,128)S(1)}, u32[]{:S(2)}, u32[]{:S(2)}) async-start(f32[16,8,384]{2,1,0:T(8,128)} %get-tuple-element.22), calls=%async_computation | async-start | bytes 393216 | tf_op jit(solution)/shard_map/all_to_all | solution.py:475
  21.5 0.0 copy-done.12
  21.6 0.0 copy-start.6
  21.6 0.0 copy-start.7
  21.6 0.0 copy-start.8
  21.6 0.0 copy-start.9
  21.6 7.9 %all-to-all-done.received_ref = f32[16,8,384]{2,1,0:T(8,128)S(1)} async-done(((f32[16,8,384]{2,1,0:T(8,128)}), f32[16,8,384]{2,1,0:T(8,128)S(1)}, u32[]{:S(2)}, u32[]{:S(2)}) %all-to-all-start) | async-done | bytes 196640 | tf_op jit(solution)/shard_map/all_to_all | solution.py:475
  29.6 0.0 copy-done.6
  29.6 0.0 copy-done.7
  29.6 0.0 copy-done.8
  29.6 0.0 copy-done.9
  29.6 0.0 copy-start.3
  29.6 0.0 copy-start.4
  29.6 0.0 copy-start.5
  29.6 1.8 %track.4 = f32[16,8,384]{2,1,0:T(8,128)} custom-call(f32[16,8,384]{2,1,0:T(8,128)S(1)} %all-to-all-done.received_ref, f32[6,4,16,256]{3,2,1,0:T(8,128)S(1)} %slice.18.table_ref, bf16[128,256]{1,0:T(8,128)(2,1)S(1)} %copy-done.9, bf16[128,256]{1,0:T(8,128)(2,1)S(1)} %copy-done.8, bf16[128,256]{1,0:T(8,128)(2,1)S(1)} %copy-done.7, bf16[128,256]{1,0:T(8,128)(2,1)S(1)} %copy-done.6), custom_call_target="tpu_custom_call" | custom-call | tf_op jit(solution)/shard_map/track/pallas_call | solution.py:463
  31.4 4.1 %all-to-all-start.1 = ((f32[16,8,384]{2,1,0:T(8,128)}), f32[16,8,384]{2,1,0:T(8,128)S(1)}, u32[]{:S(2)}, u32[]{:S(2)}) async-start(f32[16,8,384]{2,1,0:T(8,128)} %track.4), calls=%async_computation.1 | async-start | bytes 393216 | tf_op jit(solution)/shard_map/all_to_all | solution.py:475
  35.5 0.0 copy-done.13
  35.5 0.1 slice.17
  35.6 0.1 subtract_multiply_fusion
  35.7 0.1 stack.15.coef_ref
  35.8 7.8 %all-to-all-done.1.received_ref = f32[16,8,384]{2,1,0:T(8,128)S(1)} async-done(((f32[16,8,384]{2,1,0:T(8,128)}), f32[16,8,384]{2,1,0:T(8,128)S(1)}, u32[]{:S(2)}, u32[]{:S(2)}) %all-to-all-start.1) | async-done | bytes 196640 | tf_op jit(solution)/shard_map/all_to_all | solution.py:475
  43.5 0.0 copy-done.3
  43.5 0.0 copy-done.4
  43.5 0.0 copy-done.5
  43.5 0.0 copy-done.1
  43.5 0.0 copy-done.10
  43.5 1.7 %step.4 = (f32[3,4,8,256]{3,2,1,0:T(8,128)}, f32[3,4,8,256]{3,2,1,0:T(8,128)S(1)}, f32[3,4,8,256]{3,2,1,0:T(8,128)S(1)}, f32[12,256]{1,0:T(8,128)S(1)}, f32[12,2...) custom-call(s32[2]{0:T(128)S(1)} %pad_add_fusion.place_ref, f32[4,8]{1,0:T(4,128)S(1)} %stack.15.coef_ref, ...), custom_call_target="tpu_custom_call" | custom-call | tf_op jit(solution)/shard_map/step/pallas_call | solution.py:463
  45.2 11.7 %all_to_all.40.received_ref = f32[16,8,384]{2,1,0:T(8,128)S(1)} all-to-all(f32[16,8,384]{2,1,0:T(8,128)S(1)} %get-tuple-element.26), channel_id=1, replica_groups=mesh['run'=2,'gx'=4,'gy'=4] {'gx','gy'}, dimensions={0} | all-to-all | bytes 393216 | tf_op jit(solution)/shard_map/all_to_all | solution.py:475
  57.0 1.8 %track.5 = f32[16,8,384]{2,1,0:T(8,128)} custom-call(f32[16,8,384]{2,1,0:T(8,128)S(1)} %all_to_all.40.received_ref, f32[6,4,16,256]{3,2,1,0:T(8,128)S(1)} %slice.18.table_ref, bf16[128,256]{1,0:T(8,128)(2,1)S(1)} %copy-done.9, bf16[128,256]{1,0:T(8,128)(2,1)S(1)} %copy-done.8, bf16[128,256]{1,0:T(8,128)(2,1)S(1)} %copy-done.7, bf16[128,256]{1,0:T(8,128)(2,1)S(1)} %copy-done.6), custom_call_target="tpu_custom_call" | custom-call | tf_op jit(solution)/shard_map/track/pallas_call | solution.py:463
  58.8 3.9 %all-to-all-start.3 = ((f32[16,8,384]{2,1,0:T(8,128)}), f32[16,8,384]{2,1,0:T(8,128)S(1)}, u32[]{:S(2)}, u32[]{:S(2)}) async-start(f32[16,8,384]{2,1,0:T(8,128)} %track.5), calls=%async_computation.3 | async-start | bytes 393216 | tf_op jit(solution)/shard_map/all_to_all | solution.py:475
  62.7 3.8 %collective-permute-start.1 = (f32[12,256]{1,0:T(8,128)S(1)}, f32[12,256]{1,0:T(8,128)S(1)}, u32[]{:S(2)}, u32[]{:S(2)}) collective-permute-start(f32[12,256]{1,0:T(8,128)S(1)} %get-tuple-element.28), channel_id=1, source_target_pairs={{0,1},{1,2},{2,3},{3,4},{4,5},{5,6},{6,7},{7,8},{8,9},{9,10},{10,1... | collective-permute-start | bytes 36872 | tf_op jit(solution)/shard_map/ppermute | solution.py:21
  66.6 1.3 collective-permute-start.2
  67.9 0.1 collective-permute-done.1.before_ref
  68.0 4.2 %collective-permute-done.2.after_ref = f32[12,256]{1,0:T(8,128)S(1)} collective-permute-done((f32[12,256]{1,0:T(8,128)S(1)}, f32[12,256]{1,0:T(8,128)S(1)}, u32[]{:S(2)}, u32[]{:S(2)}) %collective-permute-start.2) | collective-permute-done | bytes 12320 | tf_op jit(solution)/shard_map/ppermute | solution.py:21
  72.2 0.0 all-to-all-done.3.received_ref
  72.2 1.5 %step.5 = (f32[3,4,8,256]{3,2,1,0:T(8,128)S(1)}, f32[3,4,8,256]{3,2,1,0:T(8,128)S(1)}, f32[12,256]{1,0:T(8,128)S(1)}, f32[12,256]{1,0:T(8,128)S(1)}, f32[16,8,384]{2,1,0:T(8,128)S(1)}) custom-call(s32[2]{0:T(128)S(1)} %pad_add_fusion.place_ref, f32[4,8]{1,0:T(4,128)S(1)} %stack.15.coef_ref, f32[16,8,384]{2,1,0:T(8,128)S(1)} %all-to-all-done.3.received_ref, ...), custom_call_target="tpu_custom_call" | custom-call | tf_op jit(solution)/shard_map/step/pallas_call | solution.py:463
  73.7 14.3 %all_to_all.41.received_ref = f32[16,8,384]{2,1,0:T(8,128)S(1)} all-to-all(f32[16,8,384]{2,1,0:T(8,128)S(1)} %get-tuple-element.31), channel_id=1, replica_groups=mesh['run'=2,'gx'=4,'gy'=4] {'gx','gy'}, dimensions={0} | all-to-all | bytes 393216 | tf_op jit(solution)/shard_map/all_to_all | solution.py:475
  88.0 1.8 %track.6 = f32[16,8,384]{2,1,0:T(8,128)} custom-call(f32[16,8,384]{2,1,0:T(8,128)S(1)} %all_to_all.41.received_ref, f32[6,4,16,256]{3,2,1,0:T(8,128)S(1)} %slice.18.table_ref, bf16[128,256]{1,0:T(8,128)(2,1)S(1)} %copy-done.9, bf16[128,256]{1,0:T(8,128)(2,1)S(1)} %copy-done.8, bf16[128,256]{1,0:T(8,128)(2,1)S(1)} %copy-done.7, bf16[128,256]{1,0:T(8,128)(2,1)S(1)} %copy-done.6), custom_call_target="tpu_custom_call" | custom-call | tf_op jit(solution)/shard_map/track/pallas_call | solution.py:463
  89.8 3.9 %all-to-all-start.5 = ((f32[16,8,384]{2,1,0:T(8,128)}), f32[16,8,384]{2,1,0:T(8,128)S(1)}, u32[]{:S(2)}, u32[]{:S(2)}) async-start(f32[16,8,384]{2,1,0:T(8,128)} %track.6), calls=%async_computation.5 | async-start | bytes 393216 | tf_op jit(solution)/shard_map/all_to_all | solution.py:475
  93.8 3.8 %collective-permute-start.3 = (f32[12,256]{1,0:T(8,128)S(1)}, f32[12,256]{1,0:T(8,128)S(1)}, u32[]{:S(2)}, u32[]{:S(2)}) collective-permute-start(f32[12,256]{1,0:T(8,128)S(1)} %get-tuple-element.33), channel_id=1, source_target_pairs={{0,1},{1,2},{2,3},{3,4},{4,5},{5,6},{6,7},{7,8},{8,9},{9,10},{10,1... | collective-permute-start | bytes 36872 | tf_op jit(solution)/shard_map/ppermute | solution.py:21
  97.6 1.3 collective-permute-start.4
  98.9 0.1 collective-permute-done.3.before_ref
  99.0 4.2 %collective-permute-done.4.after_ref = f32[12,256]{1,0:T(8,128)S(1)} collective-permute-done((f32[12,256]{1,0:T(8,128)S(1)}, f32[12,256]{1,0:T(8,128)S(1)}, u32[]{:S(2)}, u32[]{:S(2)}) %collective-permute-start.4) | collective-permute-done | bytes 12320 | tf_op jit(solution)/shard_map/ppermute | solution.py:21
  103.2 0.0 all-to-all-done.5.received_ref
  103.2 1.5 %step.6 = (f32[3,4,8,256]{3,2,1,0:T(8,128)S(1)}, f32[3,4,8,256]{3,2,1,0:T(8,128)S(1)}, f32[12,256]{1,0:T(8,128)S(1)}, f32[12,256]{1,0:T(8,128)S(1)}, f32[16,8,384]{2,1,0:T(8,128)S(1)}) custom-call(s32[2]{0:T(128)S(1)} %pad_add_fusion.place_ref, f32[4,8]{1,0:T(4,128)S(1)} %stack.15.coef_ref, f32[16,8,384]{2,1,0:T(8,128)S(1)} %all-to-all-done.5.received_ref, ...), custom_call_target="tpu_custom_call" | custom-call | tf_op jit(solution)/shard_map/step/pallas_call | solution.py:463
  104.8 14.3 %all_to_all.42.received_ref = f32[16,8,384]{2,1,0:T(8,128)S(1)} all-to-all(f32[16,8,384]{2,1,0:T(8,128)S(1)} %get-tuple-element.36), channel_id=1, replica_groups=mesh['run'=2,'gx'=4,'gy'=4] {'gx','gy'}, dimensions={0} | all-to-all | bytes 393216 | tf_op jit(solution)/shard_map/all_to_all | solution.py:475
  119.1 1.8 %track.7 = f32[16,8,384]{2,1,0:T(8,128)} custom-call(f32[16,8,384]{2,1,0:T(8,128)S(1)} %all_to_all.42.received_ref, f32[6,4,16,256]{3,2,1,0:T(8,128)S(1)} %slice.18.table_ref, bf16[128,256]{1,0:T(8,128)(2,1)S(1)} %copy-done.9, bf16[128,256]{1,0:T(8,128)(2,1)S(1)} %copy-done.8, bf16[128,256]{1,0:T(8,128)(2,1)S(1)} %copy-done.7, bf16[128,256]{1,0:T(8,128)(2,1)S(1)} %copy-done.6), custom_call_target="tpu_custom_call" | custom-call | tf_op jit(solution)/shard_map/track/pallas_call | solution.py:463
  120.9 3.9 %all-to-all-start.7 = ((f32[16,8,384]{2,1,0:T(8,128)}), f32[16,8,384]{2,1,0:T(8,128)S(1)}, u32[]{:S(2)}, u32[]{:S(2)}) async-start(f32[16,8,384]{2,1,0:T(8,128)} %track.7), calls=%async_computation.7 | async-start | bytes 393216 | tf_op jit(solution)/shard_map/all_to_all | solution.py:475
  124.8 3.8 %collective-permute-start.5 = (f32[12,256]{1,0:T(8,128)S(1)}, f32[12,256]{1,0:T(8,128)S(1)}, u32[]{:S(2)}, u32[]{:S(2)}) collective-permute-start(f32[12,256]{1,0:T(8,128)S(1)} %get-tuple-element.38), channel_id=1, source_target_pairs={{0,1},{1,2},{2,3},{3,4},{4,5},{5,6},{6,7},{7,8},{8,9},{9,10},{10,1... | collective-permute-start | bytes 36872 | tf_op jit(solution)/shard_map/ppermute | solution.py:21
  128.7 1.3 collective-permute-start.6
  130.0 0.1 collective-permute-done.5.before_ref
  130.1 4.2 %collective-permute-done.6.after_ref = f32[12,256]{1,0:T(8,128)S(1)} collective-permute-done((f32[12,256]{1,0:T(8,128)S(1)}, f32[12,256]{1,0:T(8,128)S(1)}, u32[]{:S(2)}, u32[]{:S(2)}) %collective-permute-start.6) | collective-permute-done | bytes 12320 | tf_op jit(solution)/shard_map/ppermute | solution.py:21
  134.3 0.0 all-to-all-done.7.received_ref
  134.3 1.7 %step.7 = f32[3,4,8,256]{3,2,1,0:T(8,128)} custom-call(s32[2]{0:T(128)S(1)} %pad_add_fusion.place_ref, f32[4,8]{1,0:T(4,128)S(1)} %stack.15.coef_ref, f32[16,8,384]{2,1,0:T(8,128)S(1)} %all-to-all-done.7.received_ref, f32[3,4,8,256]{3,2,1,0:T(8,128)S(1)} %get-tuple-element.37.state_ref, f32[12,256]{1,0:T(8,128)S(1)} %collective-permute-done.5.before_ref, ...), custom_call_target="tpu_custom_call" | custom-call | tf_op jit(solution)/shard_map/step/pallas_call | solution.py:463
  (6 shorter events, 0.0 us)
Async XLA Ops:
  0.6 8.0 %collective-permute-start = (f32[3,4,8,256]{3,2,1,0:T(8,128)}, f32[3,4,8,256]{3,2,1,0:T(8,128)S(1)}, u32[]{:S(2)}, u32[]{:S(2)}) collective-permute-start(f32[3,4,8,256]{3,2,1,0:T(8,128)} %magnet_ref.1), channel_id=1, source_target_pairs={{1,0},{2,1},{3,2},{4,3},{5,4},{6,5},{7,6},{8,7},{9,8},{10,9},{11,1... | collective-permute-start | bytes 294920 | tf_op jit(solution)/shard_map/ppermute | solution.py:21
  8.6 1.0 copy-start
  9.5 0.9 copy-start.2
  10.5 0.9 copy-start.11
  11.4 10.2 %copy-start.12 = (f32[6,7,16,256]{3,2,1,0:T(8,128)S(1)}, f32[6,7,16,256]{3,2,1,0:T(8,128)}, u32[]{:S(2)}) copy-start(f32[6,7,16,256]{3,2,1,0:T(8,128)} %param.17) | copy-start | bytes 2064388
  13.1 16.4 %all-to-all-start = ((f32[16,8,384]{2,1,0:T(8,128)}), f32[16,8,384]{2,1,0:T(8,128)S(1)}, u32[]{:S(2)}, u32[]{:S(2)}) async-start(f32[16,8,384]{2,1,0:T(8,128)} %get-tuple-element.22), calls=%async_computation | async-start | bytes 393216 | tf_op jit(solution)/shard_map/all_to_all | solution.py:475
  21.6 8.0 %copy-start.6 = (bf16[128,256]{1,0:T(8,128)(2,1)S(1)}, bf16[128,256]{1,0:T(8,128)(2,1)}, u32[]{:S(2)}) copy-start(bf16[128,256]{1,0:T(8,128)(2,1)} %constant.34.clone.wi_low) | copy-start | bytes 196612
  21.6 8.0 %copy-start.7 = (bf16[128,256]{1,0:T(8,128)(2,1)S(1)}, bf16[128,256]{1,0:T(8,128)(2,1)}, u32[]{:S(2)}) copy-start(bf16[128,256]{1,0:T(8,128)(2,1)} %constant.33.clone.wi_high) | copy-start | bytes 196612
  21.6 8.0 %copy-start.8 = (bf16[128,256]{1,0:T(8,128)(2,1)S(1)}, bf16[128,256]{1,0:T(8,128)(2,1)}, u32[]{:S(2)}) copy-start(bf16[128,256]{1,0:T(8,128)(2,1)} %constant.32.clone.wf_low) | copy-start | bytes 196612
  21.6 8.0 %copy-start.9 = (bf16[128,256]{1,0:T(8,128)(2,1)S(1)}, bf16[128,256]{1,0:T(8,128)(2,1)}, u32[]{:S(2)}) copy-start(bf16[128,256]{1,0:T(8,128)(2,1)} %constant.31.clone.wf_high) | copy-start | bytes 196612
  29.6 13.9 %copy-start.3 = (bf16[256,512]{1,0:T(8,128)(2,1)S(1)}, bf16[256,512]{1,0:T(8,128)(2,1)}, u32[]{:S(2)}) copy-start(bf16[256,512]{1,0:T(8,128)(2,1)} %constant.29.clone.refs_0_.refs_2_) | copy-start | bytes 786436
  29.6 13.9 %copy-start.4 = (bf16[512,256]{1,0:T(8,128)(2,1)S(1)}, bf16[512,256]{1,0:T(8,128)(2,1)}, u32[]{:S(2)}) copy-start(bf16[512,256]{1,0:T(8,128)(2,1)} %constant.36.clone.refs_1_) | copy-start | bytes 786436
  29.6 13.9 %copy-start.5 = (bf16[512,256]{1,0:T(8,128)(2,1)S(1)}, bf16[512,256]{1,0:T(8,128)(2,1)}, u32[]{:S(2)}) copy-start(bf16[512,256]{1,0:T(8,128)(2,1)} %constant.35.clone.refs_0_) | copy-start | bytes 786436
  31.4 4.1 %copy-start.13 = (f32[4,5]{1,0:T(4,128)S(1)}, f32[4,5]{1,0:T(4,128)}, u32[]{:S(2)}) copy-start(f32[4,5]{1,0:T(4,128)} %param.16) | copy-start | bytes 244
  31.4 12.1 %copy-start.1 = (bf16[256,512]{1,0:T(8,128)(2,1)S(1)}, bf16[256,512]{1,0:T(8,128)(2,1)}, u32[]{:S(2)}) copy-start(bf16[256,512]{1,0:T(8,128)(2,1)} %constant.30.clone.refs_1_.refs_3_) | copy-start | bytes 786436
  31.4 12.1 %all-to-all-start.1 = ((f32[16,8,384]{2,1,0:T(8,128)}), f32[16,8,384]{2,1,0:T(8,128)S(1)}, u32[]{:S(2)}, u32[]{:S(2)}) async-start(f32[16,8,384]{2,1,0:T(8,128)} %track.4), calls=%async_computation.1 | async-start | bytes 393216 | tf_op jit(solution)/shard_map/all_to_all | solution.py:475
  35.7 7.9 %copy-start.10 = (s32[8,256]{1,0:T(8,128)S(1)}, s32[8,256]{1,0:T(8,128)}, u32[]{:S(2)}) copy-start(s32[8,256]{1,0:T(8,128)} %region_ref.7) | copy-start | bytes 24580
  58.8 13.4 %all-to-all-start.3 = ((f32[16,8,384]{2,1,0:T(8,128)}), f32[16,8,384]{2,1,0:T(8,128)S(1)}, u32[]{:S(2)}, u32[]{:S(2)}) async-start(f32[16,8,384]{2,1,0:T(8,128)} %track.5), calls=%async_computation.3 | async-start | bytes 393216 | tf_op jit(solution)/shard_map/all_to_all | solution.py:475
  62.7 5.3 %collective-permute-start.1 = (f32[12,256]{1,0:T(8,128)S(1)}, f32[12,256]{1,0:T(8,128)S(1)}, u32[]{:S(2)}, u32[]{:S(2)}) collective-permute-start(f32[12,256]{1,0:T(8,128)S(1)} %get-tuple-element.28), channel_id=1, source_target_pairs={{0,1},{1,2},{2,3},{3,4},{4,5},{5,6},{6,7},{7,8},{8,9},{9,10},{10,1... | collective-permute-start | bytes 36872 | tf_op jit(solution)/shard_map/ppermute | solution.py:21
  66.6 5.6 %collective-permute-start.2 = (f32[12,256]{1,0:T(8,128)S(1)}, f32[12,256]{1,0:T(8,128)S(1)}, u32[]{:S(2)}, u32[]{:S(2)}) collective-permute-start(f32[12,256]{1,0:T(8,128)S(1)} %get-tuple-element.29), channel_id=1, source_target_pairs={{1,0},{2,1},{3,2},{4,3},{5,4},{6,5},{7,6},{8,7},{9,8},{10,9},{11,1... | collective-permute-start | bytes 36872 | tf_op jit(solution)/shard_map/ppermute | solution.py:21
  89.8 13.4 %all-to-all-start.5 = ((f32[16,8,384]{2,1,0:T(8,128)}), f32[16,8,384]{2,1,0:T(8,128)S(1)}, u32[]{:S(2)}, u32[]{:S(2)}) async-start(f32[16,8,384]{2,1,0:T(8,128)} %track.6), calls=%async_computation.5 | async-start | bytes 393216 | tf_op jit(solution)/shard_map/all_to_all | solution.py:475
  93.8 5.3 %collective-permute-start.3 = (f32[12,256]{1,0:T(8,128)S(1)}, f32[12,256]{1,0:T(8,128)S(1)}, u32[]{:S(2)}, u32[]{:S(2)}) collective-permute-start(f32[12,256]{1,0:T(8,128)S(1)} %get-tuple-element.33), channel_id=1, source_target_pairs={{0,1},{1,2},{2,3},{3,4},{4,5},{5,6},{6,7},{7,8},{8,9},{9,10},{10,1... | collective-permute-start | bytes 36872 | tf_op jit(solution)/shard_map/ppermute | solution.py:21
  97.6 5.6 %collective-permute-start.4 = (f32[12,256]{1,0:T(8,128)S(1)}, f32[12,256]{1,0:T(8,128)S(1)}, u32[]{:S(2)}, u32[]{:S(2)}) collective-permute-start(f32[12,256]{1,0:T(8,128)S(1)} %get-tuple-element.34), channel_id=1, source_target_pairs={{1,0},{2,1},{3,2},{4,3},{5,4},{6,5},{7,6},{8,7},{9,8},{10,9},{11,1... | collective-permute-start | bytes 36872 | tf_op jit(solution)/shard_map/ppermute | solution.py:21
  120.9 13.4 %all-to-all-start.7 = ((f32[16,8,384]{2,1,0:T(8,128)}), f32[16,8,384]{2,1,0:T(8,128)S(1)}, u32[]{:S(2)}, u32[]{:S(2)}) async-start(f32[16,8,384]{2,1,0:T(8,128)} %track.7), calls=%async_computation.7 | async-start | bytes 393216 | tf_op jit(solution)/shard_map/all_to_all | solution.py:475
  124.8 5.3 %collective-permute-start.5 = (f32[12,256]{1,0:T(8,128)S(1)}, f32[12,256]{1,0:T(8,128)S(1)}, u32[]{:S(2)}, u32[]{:S(2)}) collective-permute-start(f32[12,256]{1,0:T(8,128)S(1)} %get-tuple-element.38), channel_id=1, source_target_pairs={{0,1},{1,2},{2,3},{3,4},{4,5},{5,6},{6,7},{7,8},{8,9},{9,10},{10,1... | collective-permute-start | bytes 36872 | tf_op jit(solution)/shard_map/ppermute | solution.py:21
  128.7 5.6 %collective-permute-start.6 = (f32[12,256]{1,0:T(8,128)S(1)}, f32[12,256]{1,0:T(8,128)S(1)}, u32[]{:S(2)}, u32[]{:S(2)}) collective-permute-start(f32[12,256]{1,0:T(8,128)S(1)} %get-tuple-element.39), channel_id=1, source_target_pairs={{1,0},{2,1},{3,2},{4,3},{5,4},{6,5},{7,6},{8,7},{9,8},{10,9},{11,1... | collective-permute-start | bytes 36872 | tf_op jit(solution)/shard_map/ppermute | solution.py:21
where the time goes:
time: 137 us; the launch traced here: 136 us
  starting transfers between devices  40.9 us (30%)
  blocking collectives  40.3 us (29%)
  waiting for transfers between devices  34.6 us (25%)
  Pallas kernels  15.4 us (11%)
  local copies, waits for them, and re-layouts  3.05 us (2%)
  between operations  1.52 us (1%)
    all_to_all x3, blocking collectives, exchange(): lax.all_to_all(blocks, ('gx', 'gy'), split_axis=0, concat_axis=0, tiled=T...  40.3 us
    all_to_all x5, starting transfers between devices, exchange(): lax.all_to_all(blocks, ('gx', 'gy'), split_axis=0, concat_axis=0, tiled=T...  24.3 us
    ppermute x7, waiting for transfers between devices, passed_along(): lax.ppermute(value, axis, [(source, source + steps) for source in range(l...  18.9 us
    ppermute x7, starting transfers between devices, passed_along(): lax.ppermute(value, axis, [(source, source + steps) for source in range(l...  16.6 us
    all_to_all x5, waiting for transfers between devices, exchange(): lax.all_to_all(blocks, ('gx', 'gy'), split_axis=0, concat_axis=0, tiled=T...  15.7 us
    pallas_call x9, Pallas kernels, call(): pl.pallas_call(body, name=name, out_shape=[jax.ShapeDtypeStruct(s, jnp.fl...  15.4 us
    unnamed x28, local copies, waits for them, and re-layouts  2.85 us
  transfers between devices with their start and end apart: 12, of which 9 were waited for; matrix products, arithmetic and copies ran while one was open for 0% of the time, Pallas kernels for 0%

commit v1 on v0

--- a/solution.py
+++ b/solution.py
@@ -215,7 +215,7 @@
     table = np.asarray(table, np.float64).astype(np.float32)
     high = table.astype(jnp.bfloat16)
     low = (table - high.astype(np.float32)).astype(jnp.bfloat16)
-    return (high, low)
+    return np.stack([high, low])
 
 
 def angle_table(rows, cols, length):
@@ -270,11 +270,11 @@
     return results
 
 
-def send_forward(cells, forward_refs, send_ref, devices):
+def send_forward(cells, forward_ref, send_ref, devices):
     slab_rows = send_ref.shape[1]
-    size = 2 * forward_refs[0].shape[0] // devices
+    size = 2 * forward_ref.shape[1] // devices
     per_tile = lanes // size
-    spectrum = dot_halves(halves(cells), (forward_refs[0][...], forward_refs[1][...]))
+    spectrum = dot_halves(halves(cells), (forward_ref[0], forward_ref[1]))
     fields = cells.shape[0] // slab_rows
     for a in range(fields // per_tile):
         for q in range(devices // per_tile):
@@ -286,12 +286,11 @@
                 send_ref[q * per_tile + b, :, a * lanes : (a + 1) * lanes] = block
 
 
-def take_inverse(received_ref, inverse_refs, rows_ref):
+def take_inverse(received_ref, inverse_ref, rows_ref, fields):
     devices, slab_rows, width = received_ref.shape
-    size = inverse_refs[0].shape[0] // devices
+    size = inverse_ref.shape[1] // devices
     per_tile = lanes // size
-    fields = width // size
-    for a in range(fields // per_tile):
+    for a in range(width // lanes):
         for q in range(devices // per_tile):
             blocks = [
                 received_ref[q * per_tile + b, :, a * lanes : (a + 1) * lanes] for b in range(per_tile)
@@ -299,12 +298,16 @@
             for b, block in enumerate(turn_blocks(blocks, size)):
                 row = (a * per_tile + b) * slab_rows
                 rows_ref[row : row + slab_rows, q * lanes : (q + 1) * lanes] = block
-    return dot_halves(halves(rows_ref[...]), (inverse_refs[0][...], inverse_refs[1][...]))
-
-
-def window_kernel(devices, place_ref, magnet_ref, following_ref, *refs):
-    forward_refs = refs[:2]
-    initial_ref, before_ref, after_ref, send_ref, joined_ref, moved_ref = refs[2:]
+    return dot_halves(halves(rows_ref[...]), (inverse_ref[0], inverse_ref[1]))
+
+
+def first_kernel(devices, magnet_ref, forward_ref, send_ref):
+    components, layers, slab_rows, width = magnet_ref.shape
+    cells = magnet_ref[...].reshape(components * layers * slab_rows, width)
+    send_forward(cells, forward_ref, send_ref, devices)
+
+
+def window_rows(devices, place_ref, magnet_ref, following_ref, initial_ref, before_ref, after_ref, joined_ref, moved_ref):
     components, layers, slab_rows, width = magnet_ref.shape
     fields = components * layers
     position = place_ref[0]
@@ -312,7 +315,6 @@
     limit = devices * slab_rows - offset - position * slab_rows
     joined_ref[:, 0:slab_rows, :] = magnet_ref[...].reshape(fields, slab_rows, width)
     joined_ref[:, slab_rows : 2 * slab_rows, :] = following_ref[...].reshape(fields, slab_rows, width)
-
     for choice in range(1, slab_rows):
 
         @pl.when(offset == choice)
@@ -328,20 +330,52 @@
     rows = moved_ref[...]
     cell = lax.broadcasted_iota(jnp.int32, rows.shape, 1)
     state = filled(rows, cell, lax.broadcasted_iota(jnp.int32, rows.shape, 0))
+    initial_ref[...] = state.reshape(components, layers, slab_rows, width)
     edge = lax.broadcasted_iota(jnp.int32, (fields, width), 0)
-    before_ref[...] = filled(before_ref[...], jnp.full((fields, width), -1, jnp.int32), edge)
-    after_ref[...] = filled(after_ref[...], jnp.full((fields, width), slab_rows, jnp.int32), edge)
-    initial_ref[...] = state.reshape(components, layers, slab_rows, width)
-    send_forward(state.reshape(fields * slab_rows, width), forward_refs, send_ref, devices)
-
-
-def track_kernel(received_ref, table_ref, wf_high, wf_low, wi_high, wi_low, send_ref, spectrum_ref, product_ref):
+    before = filled(before_ref[...], jnp.full((fields, width), -1, jnp.int32), edge)
+    after = filled(after_ref[...], jnp.full((fields, width), slab_rows, jnp.int32), edge)
+    first = jnp.broadcast_to(position, (fields, width)) == 0
+    last = jnp.broadcast_to(position, (fields, width)) == devices - 1
+    for f in range(fields):
+        c, z = divmod(f, layers)
+        own = initial_ref[c, z]
+        before_ref[f : f + 1, :] = jnp.where(first[0:1], own[0:1], before[f : f + 1])
+        after_ref[f : f + 1, :] = jnp.where(last[0:1], own[slab_rows - 1 :], after[f : f + 1])
+
+
+def track_kernel(stage, fields, *refs):
+    refs = list(refs)
+    place_ref, fill_ref = [refs.pop(0), refs.pop(0)] if stage == 0 else (None, None)
+    received_ref, table_ref, wf_ref, wi_ref, send_ref, spectrum_ref, product_ref = refs[:7]
     devices, slab_rows, width = received_ref.shape
     components = 3
     layers, local_freq = table_ref.shape[1:3]
     track = devices * slab_rows
-    flat = received_ref[...].reshape(track, width).T
-    spectrum_ref[...] = dot_halves(halves(flat), (wf_high[...], wf_low[...]))
+    flat = received_ref[...].reshape(track, width)
+    if stage == 0:
+        joined_ref, moved_ref = refs[7:]
+        joined_ref[0:track, :] = flat
+        joined_ref[track : track + slab_rows, :] = jnp.broadcast_to(fill_ref[place_ref[0]], (slab_rows, width))
+        for choice in range(1, slab_rows):
+
+            @pl.when(place_ref[1] == choice)
+            def move():
+                moved_ref[...] = joined_ref[choice : choice + track, :]
+
+        flat = moved_ref[...]
+    else:
+        tiles = width // lanes
+        for p in range(devices):
+            lower = flat[max(p * slab_rows - 1, 0)]
+            upper = flat[min(p * slab_rows + slab_rows, track - 1)]
+            for a in range(tiles):
+                for k, line in enumerate((lower, upper)):
+                    value = line[a * lanes : (a + 1) * lanes].reshape(1, lanes)
+                    send_ref[p, k * tiles + a : k * tiles + a + 1, width : width + lanes] = value * float(2 * track)
+            if 2 * tiles < slab_rows:
+                rest = slab_rows - 2 * tiles
+                send_ref[p, 2 * tiles : slab_rows, width : width + lanes] = jnp.zeros((rest, lanes), jnp.float32)
+    spectrum_ref[...] = dot_halves(halves(flat.T), (wf_ref[0], wf_ref[1]))
     step = 8
     first_lane = lax.broadcasted_iota(jnp.int32, (step, track), 1) == 0
     for start in range(0, local_freq, step):
@@ -386,40 +420,44 @@
                             add(slot, value, term_sign * sign)
                 for slot in range(4):
                     product_ref[part(i, z, slot // 2, slot % 2)] = sums[slot]
-    result = dot_halves((wi_high[...], wi_low[...]), halves(product_ref[...]), ((1,), (1,)))
-    send_ref[...] = result.reshape(devices, slab_rows, width)
-
-
-def step_kernel(stage, devices, place_ref, coef_ref, received_ref, state_ref, before_ref, after_ref, region_ref, *refs):
+    result = dot_halves((wi_ref[0], wi_ref[1]), halves(product_ref[...]), ((1,), (1,)))
+    send_ref[:, :, 0:width] = result.reshape(devices, slab_rows, width)
+
+
+def step_kernel(stage, devices, place_ref, coef_ref, received_ref, region_ref, inverse_ref, *refs):
     refs = list(refs)
-    inverse_refs = [refs.pop(0), refs.pop(0)]
-    forward_refs = [refs.pop(0), refs.pop(0)] if stage < 3 else None
-    initial_ref = refs.pop(0) if stage > 0 else state_ref
-    sum_ref = refs.pop(0) if stage > 0 else None
-    field_ref = refs.pop(0) if stage == 0 else None
+    forward_ref = refs.pop(0) if stage < 3 else None
+    if stage == 0:
+        magnet_ref, following_ref, field_ref, initial_ref = [refs.pop(0) for _ in range(4)]
+        state_ref = initial_ref
+    else:
+        state_ref, initial_ref, sum_ref = [refs.pop(0) for _ in range(3)]
     next_ref = refs.pop(0)
     if stage < 3:
-        total_ref, head_ref, tail_ref, send_ref = [refs.pop(0) for _ in range(4)]
+        total_ref, send_ref = [refs.pop(0) for _ in range(2)]
     rows_ref = refs.pop(0)
     components, layers, slab_rows, width = state_ref.shape
-    position = place_ref[0]
-    demag = take_inverse(received_ref, inverse_refs, rows_ref)
+    if stage == 0:
+        before_ref, after_ref = refs[:2]
+        window_rows(devices, place_ref, magnet_ref, following_ref, initial_ref, *refs)
+    demag = take_inverse(received_ref, inverse_ref, rows_ref, components * layers)
+    tiles = 2 * width * components * layers // (devices * lanes)
+    per_tile = components * layers // tiles
     shape = (slab_rows, width)
     row = lax.broadcasted_iota(jnp.int32, shape, 0)
     col = lax.broadcasted_iota(jnp.int32, shape, 1)
     flow = region_ref[...].astype(jnp.float32)
-    is_first = (position == 0).astype(jnp.int32)
-    is_last = (position == devices - 1).astype(jnp.int32)
-    fields = []
-    moved = []
     for z in range(layers):
         stiffness, anisotropy, drift = (coef_ref[z, 4], coef_ref[z, 5], coef_ref[z, 6])
         m, h, g = ([], [], [])
         for c in range(components):
             f = c * layers + z
             cells = state_ref[c, z]
-            head = jnp.where(is_first == 1, cells[0:1], before_ref[f : f + 1, :])
-            tail = jnp.where(is_last == 1, cells[slab_rows - 1 : slab_rows], after_ref[f : f + 1, :])
+            if stage == 0:
+                head, tail = (before_ref[f : f + 1, :], after_ref[f : f + 1, :])
+            else:
+                line = (components * layers + f % per_tile) * slab_rows + f // per_tile
+                head, tail = (demag[line : line + 1], demag[line + tiles : line + tiles + 1])
             lower = jnp.where(row == 0, head, pltpu.roll(cells, 1, 0))
             upper = jnp.where(row == slab_rows - 1, tail, pltpu.roll(cells, slab_rows - 1, 0))
             left = jnp.where(col == 0, cells, pltpu.roll(cells, 1, 1))
@@ -447,13 +485,10 @@
                 factor = time_step if stage == 2 else 0.5 * time_step
                 value = start + factor * rate
                 next_ref[c, z] = value
-                f = c * layers + z
-                head_ref[f : f + 1, :] = value[0:1]
-                tail_ref[f : f + 1, :] = value[slab_rows - 1 : slab_rows]
                 total_ref[c, z] = rate if stage == 0 else sum_ref[c, z] + 2.0 * rate
     if stage < 3:
         cells = next_ref[...].reshape(components * layers * slab_rows, width)
-        send_forward(cells, forward_refs, send_ref, devices)
+        send_forward(cells, forward_ref, send_ref, devices)
 
 
 def call(body, name, outs, in_smem, args, scratch):
@@ -496,53 +531,52 @@
         axis=1,
     )
     table = kernel[:, layers - 1 :]
-    initial, before, after, send = call(
-        functools.partial(window_kernel, devices),
-        "window",
-        [magnet.shape, (fields, width), (fields, width), block_shape],
-        1,
-        [place, magnet, following, *forward],
-        [(fields, 2 * slab_rows, width), (fields, slab_rows, width)],
-    )
-    state = initial
-    total = None
+    ones = np.zeros((components, layers, 2, width // devices, devices))
+    sums = width_tables(width, devices, scale)[0].sum(axis=0).reshape(devices, 2, width // devices)
+    ones[2] = np.transpose(sums, (1, 2, 0))
+    fill = np.transpose(ones.reshape(row_width, devices)).reshape(devices, 1, row_width).astype(np.float32)
+    (send,) = call(
+        functools.partial(first_kernel, devices), "first", [block_shape], 0, [magnet, forward], []
+    )
+    tiles = row_width // lanes
+    per_tile = fields // tiles
+    wide_shape = (devices, slab_rows, row_width + lanes)
+    state = None
     for stage in range(4):
         received = exchange(send)
+        args = [received, table, track_forward, track_inverse]
+        scratch = [(row_width, 2 * track), (row_width, 2 * track)]
+        if stage == 0:
+            args = [place, fill] + args
+            scratch += [(track + slab_rows, row_width), (track, row_width)]
         (back,) = call(
-            track_kernel,
+            functools.partial(track_kernel, stage, fields),
             "track",
-            [block_shape],
-            0,
-            [received, table, *track_forward, *track_inverse],
-            [(row_width, 2 * track), (row_width, 2 * track)],
+            [wide_shape if stage > 0 else block_shape],
+            1 if stage == 0 else 0,
+            args,
+            scratch,
         )
         returned = exchange(back)
-        args = [place, coef, returned, state, before, after, region, *inverse]
+        args = [place, coef, returned, region, inverse]
         outs = [magnet.shape]
+        scratch = [(fields * slab_rows + (per_tile * slab_rows if stage > 0 else 0), 2 * width)]
         if stage < 3:
-            args += [*forward]
-            outs += [magnet.shape, (fields, width), (fields, width), block_shape]
+            args += [forward]
+            outs += [magnet.shape, block_shape]
         if stage > 0:
-            args += [initial, total]
+            args += [state, initial, total]
         else:
-            outs = [magnet.shape] + outs
-        results = list(
-            call(
-                functools.partial(step_kernel, stage, devices),
-                "step",
-                outs,
-                2,
-                args,
-                [(fields * slab_rows, 2 * width)],
-            )
-        )
+            args += [magnet, following]
+            outs = [magnet.shape, magnet.shape] + outs
+            scratch += [(fields, width), (fields, width), (fields, 2 * slab_rows, width), (fields, slab_rows, width)]
+        results = list(call(functools.partial(step_kernel, stage, devices), "step", outs, 2, args, scratch))
         if stage == 0:
             effective_field = results.pop(0)
+            initial = results.pop(0)
         state = results.pop(0)
         if stage < 3:
-            total, head, tail, send = results
-            before = passed_along(tail, ("gx", "gy"), 1)
-            after = passed_along(head, ("gx", "gy"), -1)
+            total, send = results
     return (state, effective_field)
 
 
@@ -558,6 +592,7 @@
     per_tile = lanes * devices // (2 * width)
     tiled = fits_tiles(devices, width) and slab_rows % 8 == 0 and track % lanes == 0 and width % lanes == 0
     tiled = tiled and components * layers % max(per_tile, 1) == 0
+    tiled = tiled and 2 * components * layers <= slab_rows * max(per_tile, 1)
     return (local_tiled if tiled else local)(magnet, window_shift, region, material, kernel)
 
 

time: 137 us -> 122 us (0.89)
  blocking collectives: 40.3 us -> 77.3 us
  starting transfers between devices: 40.9 us -> 12.8 us
  waiting for transfers between devices: 34.6 us -> 14.1 us
  Pallas kernels: 15.4 us -> 13.7 us
    all_to_all x3 -> x6, blocking collectives: 40.3 us -> 77.3 us  [exchange(): lax.all_to_all(blocks, ('gx', 'gy'), split_axis=0, concat_axis=0, tiled=T...]
    ppermute x7 -> x1, starting transfers between devices: 16.6 us -> 1.29 us  [passed_along(): lax.ppermute(value, axis, [(source, source + steps) for source in range(l...]
    all_to_all x5 -> x2, starting transfers between devices: 24.3 us -> 11.5 us  [exchange(): lax.all_to_all(blocks, ('gx', 'gy'), split_axis=0, concat_axis=0, tiled=T...]
    ppermute x7 -> x1, waiting for transfers between devices: 18.9 us -> 6.87 us  [passed_along(): lax.ppermute(value, axis, [(source, source + steps) for source in range(l...]
    all_to_all x5 -> x2, waiting for transfers between devices: 15.7 us -> 7.18 us  [exchange(): lax.all_to_all(blocks, ('gx', 'gy'), split_axis=0, concat_axis=0, tiled=T...]
    pallas_call x9, Pallas kernels: 15.4 us -> 13.7 us  [call(): pl.pallas_call(body, name=name, out_shape=[jax.ShapeDtypeStruct(s, jnp.fl...]
    unnamed x28 -> x22, local copies, waits for them, and re-layouts: 2.85 us -> 1.97 us
  transfers between devices with their start and end apart: 12 -> 3, of which waited for: 9 -> 2; matrix products, arithmetic and copies ran while one was open for 0% -> 0% of each run, Pallas kernels for 0% -> 0%
where the time goes in v1:
time: 122 us
  blocking collectives  77.3 us (63%)
  waiting for transfers between devices  14.1 us (12%)
  Pallas kernels  13.7 us (11%)
  starting transfers between devices  12.8 us (10%)
  local copies, waits for them, and re-layouts  2.17 us (2%)
  between operations  1.45 us (1%)
    all_to_all x6, blocking collectives, exchange(): lax.all_to_all(blocks, ('gx', 'gy'), split_axis=0, concat_axis=0, tiled=T...  77.3 us
    pallas_call x9, Pallas kernels, call(): pl.pallas_call(body, name=name, out_shape=[jax.ShapeDtypeStruct(s, jnp.fl...  13.7 us
    all_to_all x2, starting transfers between devices, exchange(): lax.all_to_all(blocks, ('gx', 'gy'), split_axis=0, concat_axis=0, tiled=T...  11.5 us
    all_to_all x2, waiting for transfers between devices, exchange(): lax.all_to_all(blocks, ('gx', 'gy'), split_axis=0, concat_axis=0, tiled=T...  7.18 us
    ppermute x1, waiting for transfers between devices, passed_along(): lax.ppermute(value, axis, [(source, source + steps) for source in range(l...  6.87 us
  transfers between devices with their start and end apart: 3, of which 2 were waited for; matrix products, arithmetic and copies ran while one was open for 0% of the time, Pallas kernels for 0%

profile of v1, /device:TPU:0, one launch (start us, length us, event | category | flops | bytes accessed | tf_op | source)
XLA Modules:
  0.0 121.6 jit_solution(896657324908879567)
XLA Ops:
  0.6 0.0 copy-start.1
  0.6 1.0 copy-done.1
  1.7 0.0 copy-start.5
  1.7 0.9 copy-done.5
  2.6 0.0 copy-start.9
  2.6 1.1 first.1
  3.7 7.4 %all-to-all-start = ((f32[16,8,384]{2,1,0:T(8,128)}), f32[16,8,384]{2,1,0:T(8,128)S(1)}, u32[]{:S(2)}, u32[]{:S(2)}) async-start(f32[16,8,384]{2,1,0:T(8,128)} %first.1), calls=%async_computation | async-start | bytes 393216 | tf_op jit(solution)/shard_map/all_to_all | solution.py:510
  11.7 0.0 copy-done.9
  11.8 0.0 copy-start.3
  11.8 0.0 copy-start.4
  11.8 0.0 copy-start.8
  11.8 0.1 pad_add_fusion.refs_0_.place_ref
  11.9 0.0 copy-start
  11.9 0.0 copy-start.2
  11.9 7.2 %all-to-all-done.refs_2_ = f32[16,8,384]{2,1,0:T(8,128)S(1)} async-done(((f32[16,8,384]{2,1,0:T(8,128)}), f32[16,8,384]{2,1,0:T(8,128)S(1)}, u32[]{:S(2)}, u32[]{:S(2)}) %all-to-all-start) | async-done | bytes 196640 | tf_op jit(solution)/shard_map/all_to_all | solution.py:510
  19.1 0.0 copy-done.3
  19.1 0.0 copy-done.4
  19.1 0.0 copy-done.8
  19.1 2.4 %track.4 = f32[16,8,384]{2,1,0:T(8,128)} custom-call(s32[2]{0:T(128)S(1)} %pad_add_fusion.refs_0_.place_ref, f32[16,1,384]{2,1,0:T(1,128)S(1)} %copy-done.8, f32[16,8,384]{2,1,0:T(8,128)S(1)} %all-to-all-done.refs_2_, f32[6,4,16,256]{3,2,1,0:T(8,128)S(1)} %slice.18.refs_3_.refs_1_, bf16[2,128,256]{2,1,0:T(8,128)(2,1)S(1)} %copy-done.4, ...), custom_call_target="tpu_custom_call" | custom-call | tf_op jit(solution)/shard_map/track/pallas_call | solution.py:498
  21.5 0.0 copy-start.6
  21.5 0.0 copy-start.10
  21.5 4.1 %all-to-all-start.1 = ((f32[16,8,384]{2,1,0:T(8,128)}), f32[16,8,384]{2,1,0:T(8,128)S(1)}, u32[]{:S(2)}, u32[]{:S(2)}) async-start(f32[16,8,384]{2,1,0:T(8,128)} %track.4), calls=%async_computation.1 | async-start | bytes 393216 | tf_op jit(solution)/shard_map/all_to_all | solution.py:510
  25.6 0.0 copy-done.6
  25.6 1.3 %collective-permute-start = (f32[3,4,8,256]{3,2,1,0:T(8,128)S(1)}, f32[3,4,8,256]{3,2,1,0:T(8,128)S(1)}, u32[]{:S(2)}, u32[]{:S(2)}) collective-permute-start(f32[3,4,8,256]{3,2,1,0:T(8,128)S(1)} %copy-done.6), channel_id=1, source_target_pairs={{1,0},{2,1},{3,2},{4,3},{5,4},{6,5},{7,6},{8,7},{9,8},{10,9},{11,1... | collective-permute-start | bytes 294920 | tf_op jit(solution)/shard_map/ppermute | solution.py:21
  26.9 0.0 copy-done.10
  26.9 0.1 subtract_multiply_fusion
  27.0 0.1 slice.17
  27.1 0.0 copy-start.7
  27.1 0.1 stack.15.coef_ref
  27.2 6.9 %collective-permute-done.refs_2_ = f32[3,4,8,256]{3,2,1,0:T(8,128)S(1)} collective-permute-done((f32[3,4,8,256]{3,2,1,0:T(8,128)S(1)}, f32[3,4,8,256]{3,2,1,0:T(8,128)S(1)}, u32[]{:S(2)}, u32[]{:S(2)}) %collective-permute-start) | collective-permute-done | bytes 98336 | tf_op jit(solution)/shard_map/ppermute | solution.py:21
  34.0 0.0 all-to-all-done.1.received_ref
  34.0 0.0 copy-done
  34.0 0.0 copy-done.2
  34.0 0.0 copy-done.7
  34.1 1.8 %step.4 = (f32[3,4,8,256]{3,2,1,0:T(8,128)}, f32[3,4,8,256]{3,2,1,0:T(8,128)S(1)}, f32[3,4,8,256]{3,2,1,0:T(8,128)S(1)}, f32[3,4,8,256]{3,2,1,0:T(8,128)S(1)}, f32[16,8,384]{2,1,0:T(8,128)S(1)}) custom-call(s32[2]{0:T(128)S(1)} %pad_add_fusion.refs_0_.place_ref, f32[4,8]{1,0:T(4,128)S(1)} %stack.15.coef_ref, f32[16,8,384]{2,1,0:T(8,128)S(1)} %all-to-all-done.1.received_ref, ...), custom_call_target="tpu_custom_call" | custom-call | tf_op jit(solution)/shard_map/step/pallas_call | solution.py:498
  35.8 13.9 %all_to_all.40.refs_0_ = f32[16,8,384]{2,1,0:T(8,128)S(1)} all-to-all(f32[16,8,384]{2,1,0:T(8,128)S(1)} %get-tuple-element.13), channel_id=1, replica_groups=mesh['run'=2,'gx'=4,'gy'=4] {'gx','gy'}, dimensions={0} | all-to-all | bytes 393216 | tf_op jit(solution)/shard_map/all_to_all | solution.py:510
  49.7 1.1 track.5
  50.8 13.5 %all_to_all.41.received_ref = f32[16,8,512]{2,1,0:T(8,128)S(1)} all-to-all(f32[16,8,512]{2,1,0:T(8,128)S(1)} %track.5), channel_id=1, replica_groups=mesh['run'=2,'gx'=4,'gy'=4] {'gx','gy'}, dimensions={0} | all-to-all | bytes 524288 | tf_op jit(solution)/shard_map/all_to_all | solution.py:510
  64.3 1.7 %step.5 = (f32[3,4,8,256]{3,2,1,0:T(8,128)S(1)}, f32[3,4,8,256]{3,2,1,0:T(8,128)S(1)}, f32[16,8,384]{2,1,0:T(8,128)S(1)}) custom-call(s32[2]{0:T(128)S(1)} %pad_add_fusion.refs_0_.place_ref, f32[4,8]{1,0:T(4,128)S(1)} %stack.15.coef_ref, f32[16,8,512]{2,1,0:T(8,128)S(1)} %all_to_all.41.received_ref, s32[8,256]{1,0:T(8,128)S(1)} %copy-done.7, ...), custom_call_target="tpu_custom_call" | custom-call | tf_op jit(solution)/shard_map/step/pallas_call | solution.py:498
  66.0 11.4 %all_to_all.42.refs_0_ = f32[16,8,384]{2,1,0:T(8,128)S(1)} all-to-all(f32[16,8,384]{2,1,0:T(8,128)S(1)} %get-tuple-element.17), channel_id=1, replica_groups=mesh['run'=2,'gx'=4,'gy'=4] {'gx','gy'}, dimensions={0} | all-to-all | bytes 393216 | tf_op jit(solution)/shard_map/all_to_all | solution.py:510
  77.4 1.1 track.6
  78.6 13.5 %all_to_all.43.received_ref = f32[16,8,512]{2,1,0:T(8,128)S(1)} all-to-all(f32[16,8,512]{2,1,0:T(8,128)S(1)} %track.6), channel_id=1, replica_groups=mesh['run'=2,'gx'=4,'gy'=4] {'gx','gy'}, dimensions={0} | all-to-all | bytes 524288 | tf_op jit(solution)/shard_map/all_to_all | solution.py:510
  92.1 1.7 %step.6 = (f32[3,4,8,256]{3,2,1,0:T(8,128)S(1)}, f32[3,4,8,256]{3,2,1,0:T(8,128)S(1)}, f32[16,8,384]{2,1,0:T(8,128)S(1)}) custom-call(s32[2]{0:T(128)S(1)} %pad_add_fusion.refs_0_.place_ref, f32[4,8]{1,0:T(4,128)S(1)} %stack.15.coef_ref, f32[16,8,512]{2,1,0:T(8,128)S(1)} %all_to_all.43.received_ref, s32[8,256]{1,0:T(8,128)S(1)} %copy-done.7, ...), custom_call_target="tpu_custom_call" | custom-call | tf_op jit(solution)/shard_map/step/pallas_call | solution.py:498
  93.7 11.4 %all_to_all.44.refs_0_ = f32[16,8,384]{2,1,0:T(8,128)S(1)} all-to-all(f32[16,8,384]{2,1,0:T(8,128)S(1)} %get-tuple-element.20), channel_id=1, replica_groups=mesh['run'=2,'gx'=4,'gy'=4] {'gx','gy'}, dimensions={0} | all-to-all | bytes 393216 | tf_op jit(solution)/shard_map/all_to_all | solution.py:510
  105.2 1.1 track.7
  106.3 13.5 %all_to_all.45.received_ref = f32[16,8,512]{2,1,0:T(8,128)S(1)} all-to-all(f32[16,8,512]{2,1,0:T(8,128)S(1)} %track.7), channel_id=1, replica_groups=mesh['run'=2,'gx'=4,'gy'=4] {'gx','gy'}, dimensions={0} | all-to-all | bytes 524288 | tf_op jit(solution)/shard_map/all_to_all | solution.py:510
  119.8 1.8 %step.7 = f32[3,4,8,256]{3,2,1,0:T(8,128)} custom-call(s32[2]{0:T(128)S(1)} %pad_add_fusion.refs_0_.place_ref, f32[4,8]{1,0:T(4,128)S(1)} %stack.15.coef_ref, f32[16,8,512]{2,1,0:T(8,128)S(1)} %all_to_all.45.received_ref, s32[8,256]{1,0:T(8,128)S(1)} %copy-done.7, bf16[2,512,256]{2,1,0:T(8,128)(2,1)S(1)} %copy-done, ...), custom_call_target="tpu_custom_call" | custom-call | tf_op jit(solution)/shard_map/step/pallas_call | solution.py:498
  (2 shorter events, 0.0 us)
Async XLA Ops:
  0.6 1.0 copy-start.1
  1.7 0.9 copy-start.5
  2.6 9.2 %copy-start.9 = (f32[6,7,16,256]{3,2,1,0:T(8,128)S(1)}, f32[6,7,16,256]{3,2,1,0:T(8,128)}, u32[]{:S(2)}) copy-start(f32[6,7,16,256]{3,2,1,0:T(8,128)} %param.14) | copy-start | bytes 2064388
  3.7 15.4 %all-to-all-start = ((f32[16,8,384]{2,1,0:T(8,128)}), f32[16,8,384]{2,1,0:T(8,128)S(1)}, u32[]{:S(2)}, u32[]{:S(2)}) async-start(f32[16,8,384]{2,1,0:T(8,128)} %first.1), calls=%async_computation | async-start | bytes 393216 | tf_op jit(solution)/shard_map/all_to_all | solution.py:510
  11.8 7.3 %copy-start.3 = (bf16[2,128,256]{2,1,0:T(8,128)(2,1)S(1)}, bf16[2,128,256]{2,1,0:T(8,128)(2,1)}, u32[]{:S(2)}) copy-start(bf16[2,128,256]{2,1,0:T(8,128)(2,1)} %constant.26.clone.refs_5_.refs_3_) | copy-start | bytes 393220
  11.8 7.3 %copy-start.4 = (bf16[2,128,256]{2,1,0:T(8,128)(2,1)S(1)}, bf16[2,128,256]{2,1,0:T(8,128)(2,1)}, u32[]{:S(2)}) copy-start(bf16[2,128,256]{2,1,0:T(8,128)(2,1)} %constant.25.clone.refs_4_.refs_2_) | copy-start | bytes 393220
  11.8 7.3 %copy-start.8 = (f32[16,1,384]{2,1,0:T(1,128)S(1)}, f32[16,1,384]{2,1,0:T(1,128)}, u32[]{:S(2)}) copy-start(f32[16,1,384]{2,1,0:T(1,128)} %constant.24.clone.refs_1_) | copy-start | bytes 73732
  11.9 22.1 %copy-start = (bf16[2,512,256]{2,1,0:T(8,128)(2,1)S(1)}, bf16[2,512,256]{2,1,0:T(8,128)(2,1)}, u32[]{:S(2)}) copy-start(bf16[2,512,256]{2,1,0:T(8,128)(2,1)} %constant.27.clone.inverse_ref) | copy-start | bytes 1572868
  11.9 22.1 %copy-start.2 = (bf16[2,256,512]{2,1,0:T(8,128)(2,1)S(1)}, bf16[2,256,512]{2,1,0:T(8,128)(2,1)}, u32[]{:S(2)}) copy-start(bf16[2,256,512]{2,1,0:T(8,128)(2,1)} %constant.23.clone.forward_ref.refs_0_) | copy-start | bytes 1572868
  21.5 4.1 %copy-start.6 = (f32[3,4,8,256]{3,2,1,0:T(8,128)S(1)}, f32[3,4,8,256]{3,2,1,0:T(8,128)}, u32[]{:S(2)}) copy-start(f32[3,4,8,256]{3,2,1,0:T(8,128)} %refs_1_.2) | copy-start | bytes 294916
  21.5 5.4 %copy-start.10 = (f32[4,5]{1,0:T(4,128)S(1)}, f32[4,5]{1,0:T(4,128)}, u32[]{:S(2)}) copy-start(f32[4,5]{1,0:T(4,128)} %param.13) | copy-start | bytes 244
  21.5 12.5 %all-to-all-start.1 = ((f32[16,8,384]{2,1,0:T(8,128)}), f32[16,8,384]{2,1,0:T(8,128)S(1)}, u32[]{:S(2)}, u32[]{:S(2)}) async-start(f32[16,8,384]{2,1,0:T(8,128)} %track.4), calls=%async_computation.1 | async-start | bytes 393216 | tf_op jit(solution)/shard_map/all_to_all | solution.py:510
  25.6 8.4 %collective-permute-start = (f32[3,4,8,256]{3,2,1,0:T(8,128)S(1)}, f32[3,4,8,256]{3,2,1,0:T(8,128)S(1)}, u32[]{:S(2)}, u32[]{:S(2)}) collective-permute-start(f32[3,4,8,256]{3,2,1,0:T(8,128)S(1)} %copy-done.6), channel_id=1, source_target_pairs={{1,0},{2,1},{3,2},{4,3},{5,4},{6,5},{7,6},{8,7},{9,8},{10,9},{11,1... | collective-permute-start | bytes 294920 | tf_op jit(solution)/shard_map/ppermute | solution.py:21
  27.1 7.0 %copy-start.7 = (s32[8,256]{1,0:T(8,128)S(1)}, s32[8,256]{1,0:T(8,128)}, u32[]{:S(2)}) copy-start(s32[8,256]{1,0:T(8,128)} %region_ref.7) | copy-start | bytes 24580

commit v2 on v1

--- a/solution.py
+++ b/solution.py
@@ -253,7 +253,9 @@
     def dot(a, b):
         return lax.dot_general(a, b, (dims, ((), ())), preferred_element_type=jnp.float32)
 
-    return dot(left[0], right[0]) + (dot(left[0], right[1]) + dot(left[1], right[0]))
+    rows = left[0].shape[0]
+    both = dot(jnp.concatenate([left[0], left[1]], axis=0), right[0])
+    return both[:rows] + (both[rows:] + dot(left[0], right[1]))
 
 
 def turn_blocks(blocks, size):
@@ -301,7 +303,15 @@
     return dot_halves(halves(rows_ref[...]), (inverse_ref[0], inverse_ref[1]))
 
 
-def first_kernel(devices, magnet_ref, forward_ref, send_ref):
+def first_kernel(devices, magnet_hbm, forward_hbm, send_ref, magnet_ref, forward_ref, sems):
+    copies = [
+        pltpu.make_async_copy(magnet_hbm, magnet_ref, sems.at[0]),
+        pltpu.make_async_copy(forward_hbm, forward_ref, sems.at[1]),
+    ]
+    for copy in copies:
+        copy.start()
+    for copy in copies:
+        copy.wait()
     components, layers, slab_rows, width = magnet_ref.shape
     cells = magnet_ref[...].reshape(components * layers * slab_rows, width)
     send_forward(cells, forward_ref, send_ref, devices)
@@ -535,9 +545,19 @@
     sums = width_tables(width, devices, scale)[0].sum(axis=0).reshape(devices, 2, width // devices)
     ones[2] = np.transpose(sums, (1, 2, 0))
     fill = np.transpose(ones.reshape(row_width, devices)).reshape(devices, 1, row_width).astype(np.float32)
-    (send,) = call(
-        functools.partial(first_kernel, devices), "first", [block_shape], 0, [magnet, forward], []
-    )
+    send = pl.pallas_call(
+        functools.partial(first_kernel, devices),
+        name="first",
+        out_shape=jax.ShapeDtypeStruct(block_shape, jnp.float32),
+        in_specs=[pl.BlockSpec(memory_space=pltpu.HBM)] * 2,
+        out_specs=pl.BlockSpec(memory_space=pltpu.VMEM),
+        scratch_shapes=[
+            pltpu.VMEM(magnet.shape, jnp.float32),
+            pltpu.VMEM(forward.shape, jnp.bfloat16),
+            pltpu.SemaphoreType.DMA((2,)),
+        ],
+        compiler_params=pltpu.CompilerParams(vmem_limit_bytes=24 * 1024 * 1024),
+    )(magnet, forward)
     tiles = row_width // lanes
     per_tile = fields // tiles
     wide_shape = (devices, slab_rows, row_width + lanes)

time: 122 us -> 122 us (level)
    pallas_call x9 -> x8, Pallas kernels: 13.7 us -> 12.2 us  [call(): pl.pallas_call(body, name=name, out_shape=[jax.ShapeDtypeStruct(s, jnp.fl...]
    pallas_call x0 -> x1, Pallas kernels: none -> 1.27 us  [local_tiled(): pl.pallas_call(functools.partial(first_kernel, devices), name='first', ou...]
where the time goes in v2:
time: 122 us; the launch traced here: 121 us
  blocking collectives  77.3 us (63%)
  waiting for transfers between devices  14.1 us (12%)
  Pallas kernels  13.5 us (11%)
  starting transfers between devices  12.8 us (10%)
  local copies, waits for them, and re-layouts  2.17 us (2%)
  between operations  1.45 us (1%)
    all_to_all x6, blocking collectives, exchange(): lax.all_to_all(blocks, ('gx', 'gy'), split_axis=0, concat_axis=0, tiled=T...  77.3 us
    pallas_call x8, Pallas kernels, call(): pl.pallas_call(body, name=name, out_shape=[jax.ShapeDtypeStruct(s, jnp.fl...  12.2 us
    all_to_all x2, starting transfers between devices, exchange(): lax.all_to_all(blocks, ('gx', 'gy'), split_axis=0, concat_axis=0, tiled=T...  11.5 us
    all_to_all x2, waiting for transfers between devices, exchange(): lax.all_to_all(blocks, ('gx', 'gy'), split_axis=0, concat_axis=0, tiled=T...  7.18 us
    ppermute x1, waiting for transfers between devices, passed_along(): lax.ppermute(value, axis, [(source, source + steps) for source in range(l...  6.87 us
  transfers between devices with their start and end apart: 3, of which 2 were waited for; matrix products, arithmetic and copies ran while one was open for 0% of the time, Pallas kernels for 0%

profile of v2, /device:TPU:0, one launch (start us, length us, event | category | flops | bytes accessed | tf_op | source)
XLA Modules:
  0.0 121.4 jit_solution(10868709250762607534)
XLA Ops:
  0.6 0.0 copy-start.1
  0.6 1.0 copy-done.1
  1.7 0.0 copy-start.5
  1.7 0.9 copy-done.5
  2.6 0.0 copy-start.9
  2.6 1.3 %first.1 = f32[16,8,384]{2,1,0:T(8,128)} custom-call(f32[3,4,8,256]{3,2,1,0:T(8,128)S(1)} %copy-done.5, bf16[2,256,512]{2,1,0:T(8,128)(2,1)S(1)} %copy-done.1), custom_call_target="tpu_custom_call" | custom-call | tf_op jit(solution)/shard_map/first/pallas_call | solution.py:548
  3.8 7.4 %all-to-all-start = ((f32[16,8,384]{2,1,0:T(8,128)}), f32[16,8,384]{2,1,0:T(8,128)S(1)}, u32[]{:S(2)}, u32[]{:S(2)}) async-start(f32[16,8,384]{2,1,0:T(8,128)} %first.1), calls=%async_computation | async-start | bytes 393216 | tf_op jit(solution)/shard_map/all_to_all | solution.py:520
  11.9 0.0 copy-done.9
  11.9 0.0 copy-start.3
  11.9 0.0 copy-start.4
  11.9 0.0 copy-start.8
  12.0 0.1 pad_add_fusion.refs_0_.place_ref
  12.1 0.0 copy-start
  12.1 0.0 copy-start.2
  12.1 7.2 %all-to-all-done.refs_2_ = f32[16,8,384]{2,1,0:T(8,128)S(1)} async-done(((f32[16,8,384]{2,1,0:T(8,128)}), f32[16,8,384]{2,1,0:T(8,128)S(1)}, u32[]{:S(2)}, u32[]{:S(2)}) %all-to-all-start) | async-done | bytes 196640 | tf_op jit(solution)/shard_map/all_to_all | solution.py:520
  19.3 0.0 copy-done.3
  19.3 0.0 copy-done.4
  19.3 0.0 copy-done.8
  19.3 2.3 %track.4 = f32[16,8,384]{2,1,0:T(8,128)} custom-call(s32[2]{0:T(128)S(1)} %pad_add_fusion.refs_0_.place_ref, f32[16,1,384]{2,1,0:T(1,128)S(1)} %copy-done.8, f32[16,8,384]{2,1,0:T(8,128)S(1)} %all-to-all-done.refs_2_, f32[6,4,16,256]{3,2,1,0:T(8,128)S(1)} %slice.18.refs_3_.refs_1_, bf16[2,128,256]{2,1,0:T(8,128)(2,1)S(1)} %copy-done.4, ...), custom_call_target="tpu_custom_call" | custom-call | tf_op jit(solution)/shard_map/track/pallas_call | solution.py:508
  21.6 0.0 copy-start.6
  21.6 0.0 copy-start.10
  21.6 4.1 %all-to-all-start.1 = ((f32[16,8,384]{2,1,0:T(8,128)}), f32[16,8,384]{2,1,0:T(8,128)S(1)}, u32[]{:S(2)}, u32[]{:S(2)}) async-start(f32[16,8,384]{2,1,0:T(8,128)} %track.4), calls=%async_computation.1 | async-start | bytes 393216 | tf_op jit(solution)/shard_map/all_to_all | solution.py:520
  25.7 0.0 copy-done.6
  25.7 1.3 %collective-permute-start = (f32[3,4,8,256]{3,2,1,0:T(8,128)S(1)}, f32[3,4,8,256]{3,2,1,0:T(8,128)S(1)}, u32[]{:S(2)}, u32[]{:S(2)}) collective-permute-start(f32[3,4,8,256]{3,2,1,0:T(8,128)S(1)} %copy-done.6), channel_id=1, source_target_pairs={{1,0},{2,1},{3,2},{4,3},{5,4},{6,5},{7,6},{8,7},{9,8},{10,9},{11,1... | collective-permute-start | bytes 294920 | tf_op jit(solution)/shard_map/ppermute | solution.py:21
  27.0 0.0 copy-done.10
  27.0 0.1 subtract_multiply_fusion
  27.1 0.1 slice.17
  27.2 0.0 copy-start.7
  27.2 0.1 stack.15.coef_ref
  27.3 6.9 %collective-permute-done.refs_2_ = f32[3,4,8,256]{3,2,1,0:T(8,128)S(1)} collective-permute-done((f32[3,4,8,256]{3,2,1,0:T(8,128)S(1)}, f32[3,4,8,256]{3,2,1,0:T(8,128)S(1)}, u32[]{:S(2)}, u32[]{:S(2)}) %collective-permute-start) | collective-permute-done | bytes 98336 | tf_op jit(solution)/shard_map/ppermute | solution.py:21
  34.1 0.0 all-to-all-done.1.received_ref
  34.1 0.0 copy-done
  34.1 0.0 copy-done.2
  34.1 0.0 copy-done.7
  34.2 1.7 %step.4 = (f32[3,4,8,256]{3,2,1,0:T(8,128)}, f32[3,4,8,256]{3,2,1,0:T(8,128)S(1)}, f32[3,4,8,256]{3,2,1,0:T(8,128)S(1)}, f32[3,4,8,256]{3,2,1,0:T(8,128)S(1)}, f32[16,8,384]{2,1,0:T(8,128)S(1)}) custom-call(s32[2]{0:T(128)S(1)} %pad_add_fusion.refs_0_.place_ref, f32[4,8]{1,0:T(4,128)S(1)} %stack.15.coef_ref, f32[16,8,384]{2,1,0:T(8,128)S(1)} %all-to-all-done.1.received_ref, ...), custom_call_target="tpu_custom_call" | custom-call | tf_op jit(solution)/shard_map/step/pallas_call | solution.py:508
  35.9 13.9 %all_to_all.40.refs_0_ = f32[16,8,384]{2,1,0:T(8,128)S(1)} all-to-all(f32[16,8,384]{2,1,0:T(8,128)S(1)} %get-tuple-element.13), channel_id=1, replica_groups=mesh['run'=2,'gx'=4,'gy'=4] {'gx','gy'}, dimensions={0} | all-to-all | bytes 393216 | tf_op jit(solution)/shard_map/all_to_all | solution.py:520
  49.8 1.1 track.5
  50.8 13.5 %all_to_all.41.received_ref = f32[16,8,512]{2,1,0:T(8,128)S(1)} all-to-all(f32[16,8,512]{2,1,0:T(8,128)S(1)} %track.5), channel_id=1, replica_groups=mesh['run'=2,'gx'=4,'gy'=4] {'gx','gy'}, dimensions={0} | all-to-all | bytes 524288 | tf_op jit(solution)/shard_map/all_to_all | solution.py:520
  64.3 1.6 %step.5 = (f32[3,4,8,256]{3,2,1,0:T(8,128)S(1)}, f32[3,4,8,256]{3,2,1,0:T(8,128)S(1)}, f32[16,8,384]{2,1,0:T(8,128)S(1)}) custom-call(s32[2]{0:T(128)S(1)} %pad_add_fusion.refs_0_.place_ref, f32[4,8]{1,0:T(4,128)S(1)} %stack.15.coef_ref, f32[16,8,512]{2,1,0:T(8,128)S(1)} %all_to_all.41.received_ref, s32[8,256]{1,0:T(8,128)S(1)} %copy-done.7, ...), custom_call_target="tpu_custom_call" | custom-call | tf_op jit(solution)/shard_map/step/pallas_call | solution.py:508
  65.9 11.4 %all_to_all.42.refs_0_ = f32[16,8,384]{2,1,0:T(8,128)S(1)} all-to-all(f32[16,8,384]{2,1,0:T(8,128)S(1)} %get-tuple-element.17), channel_id=1, replica_groups=mesh['run'=2,'gx'=4,'gy'=4] {'gx','gy'}, dimensions={0} | all-to-all | bytes 393216 | tf_op jit(solution)/shard_map/all_to_all | solution.py:520
  77.4 1.1 track.6
  78.4 13.5 %all_to_all.43.received_ref = f32[16,8,512]{2,1,0:T(8,128)S(1)} all-to-all(f32[16,8,512]{2,1,0:T(8,128)S(1)} %track.6), channel_id=1, replica_groups=mesh['run'=2,'gx'=4,'gy'=4] {'gx','gy'}, dimensions={0} | all-to-all | bytes 524288 | tf_op jit(solution)/shard_map/all_to_all | solution.py:520
  91.9 1.6 %step.6 = (f32[3,4,8,256]{3,2,1,0:T(8,128)S(1)}, f32[3,4,8,256]{3,2,1,0:T(8,128)S(1)}, f32[16,8,384]{2,1,0:T(8,128)S(1)}) custom-call(s32[2]{0:T(128)S(1)} %pad_add_fusion.refs_0_.place_ref, f32[4,8]{1,0:T(4,128)S(1)} %stack.15.coef_ref, f32[16,8,512]{2,1,0:T(8,128)S(1)} %all_to_all.43.received_ref, s32[8,256]{1,0:T(8,128)S(1)} %copy-done.7, ...), custom_call_target="tpu_custom_call" | custom-call | tf_op jit(solution)/shard_map/step/pallas_call | solution.py:508
  93.5 11.4 %all_to_all.44.refs_0_ = f32[16,8,384]{2,1,0:T(8,128)S(1)} all-to-all(f32[16,8,384]{2,1,0:T(8,128)S(1)} %get-tuple-element.20), channel_id=1, replica_groups=mesh['run'=2,'gx'=4,'gy'=4] {'gx','gy'}, dimensions={0} | all-to-all | bytes 393216 | tf_op jit(solution)/shard_map/all_to_all | solution.py:520
  105.0 1.1 track.7
  106.1 13.5 %all_to_all.45.received_ref = f32[16,8,512]{2,1,0:T(8,128)S(1)} all-to-all(f32[16,8,512]{2,1,0:T(8,128)S(1)} %track.7), channel_id=1, replica_groups=mesh['run'=2,'gx'=4,'gy'=4] {'gx','gy'}, dimensions={0} | all-to-all | bytes 524288 | tf_op jit(solution)/shard_map/all_to_all | solution.py:520
  119.6 1.8 %step.7 = f32[3,4,8,256]{3,2,1,0:T(8,128)} custom-call(s32[2]{0:T(128)S(1)} %pad_add_fusion.refs_0_.place_ref, f32[4,8]{1,0:T(4,128)S(1)} %stack.15.coef_ref, f32[16,8,512]{2,1,0:T(8,128)S(1)} %all_to_all.45.received_ref, s32[8,256]{1,0:T(8,128)S(1)} %copy-done.7, bf16[2,512,256]{2,1,0:T(8,128)(2,1)S(1)} %copy-done, ...), custom_call_target="tpu_custom_call" | custom-call | tf_op jit(solution)/shard_map/step/pallas_call | solution.py:508
  (2 shorter events, 0.0 us)
Async XLA Ops:
  0.6 1.0 copy-start.1
  1.7 0.9 copy-start.5
  2.6 9.3 %copy-start.9 = (f32[6,7,16,256]{3,2,1,0:T(8,128)S(1)}, f32[6,7,16,256]{3,2,1,0:T(8,128)}, u32[]{:S(2)}) copy-start(f32[6,7,16,256]{3,2,1,0:T(8,128)} %param.14) | copy-start | bytes 2064388
  3.8 15.4 %all-to-all-start = ((f32[16,8,384]{2,1,0:T(8,128)}), f32[16,8,384]{2,1,0:T(8,128)S(1)}, u32[]{:S(2)}, u32[]{:S(2)}) async-start(f32[16,8,384]{2,1,0:T(8,128)} %first.1), calls=%async_computation | async-start | bytes 393216 | tf_op jit(solution)/shard_map/all_to_all | solution.py:520
  11.9 7.3 %copy-start.3 = (bf16[2,128,256]{2,1,0:T(8,128)(2,1)S(1)}, bf16[2,128,256]{2,1,0:T(8,128)(2,1)}, u32[]{:S(2)}) copy-start(bf16[2,128,256]{2,1,0:T(8,128)(2,1)} %constant.26.clone.refs_5_.refs_3_) | copy-start | bytes 393220
  11.9 7.3 %copy-start.4 = (bf16[2,128,256]{2,1,0:T(8,128)(2,1)S(1)}, bf16[2,128,256]{2,1,0:T(8,128)(2,1)}, u32[]{:S(2)}) copy-start(bf16[2,128,256]{2,1,0:T(8,128)(2,1)} %constant.25.clone.refs_4_.refs_2_) | copy-start | bytes 393220
  11.9 7.3 %copy-start.8 = (f32[16,1,384]{2,1,0:T(1,128)S(1)}, f32[16,1,384]{2,1,0:T(1,128)}, u32[]{:S(2)}) copy-start(f32[16,1,384]{2,1,0:T(1,128)} %constant.24.clone.refs_1_) | copy-start | bytes 73732
  12.1 22.1 %copy-start = (bf16[2,512,256]{2,1,0:T(8,128)(2,1)S(1)}, bf16[2,512,256]{2,1,0:T(8,128)(2,1)}, u32[]{:S(2)}) copy-start(bf16[2,512,256]{2,1,0:T(8,128)(2,1)} %constant.27.clone.inverse_ref) | copy-start | bytes 1572868
  12.1 22.1 %copy-start.2 = (bf16[2,256,512]{2,1,0:T(8,128)(2,1)S(1)}, bf16[2,256,512]{2,1,0:T(8,128)(2,1)}, u32[]{:S(2)}) copy-start(bf16[2,256,512]{2,1,0:T(8,128)(2,1)} %constant.23.clone.forward_hbm.refs_0_) | copy-start | bytes 1572868
  21.6 4.1 %copy-start.6 = (f32[3,4,8,256]{3,2,1,0:T(8,128)S(1)}, f32[3,4,8,256]{3,2,1,0:T(8,128)}, u32[]{:S(2)}) copy-start(f32[3,4,8,256]{3,2,1,0:T(8,128)} %refs_1_.2) | copy-start | bytes 294916
  21.6 5.4 %copy-start.10 = (f32[4,5]{1,0:T(4,128)S(1)}, f32[4,5]{1,0:T(4,128)}, u32[]{:S(2)}) copy-start(f32[4,5]{1,0:T(4,128)} %param.13) | copy-start | bytes 244
  21.6 12.5 %all-to-all-start.1 = ((f32[16,8,384]{2,1,0:T(8,128)}), f32[16,8,384]{2,1,0:T(8,128)S(1)}, u32[]{:S(2)}, u32[]{:S(2)}) async-start(f32[16,8,384]{2,1,0:T(8,128)} %track.4), calls=%async_computation.1 | async-start | bytes 393216 | tf_op jit(solution)/shard_map/all_to_all | solution.py:520
  25.7 8.4 %collective-permute-start = (f32[3,4,8,256]{3,2,1,0:T(8,128)S(1)}, f32[3,4,8,256]{3,2,1,0:T(8,128)S(1)}, u32[]{:S(2)}, u32[]{:S(2)}) collective-permute-start(f32[3,4,8,256]{3,2,1,0:T(8,128)S(1)} %copy-done.6), channel_id=1, source_target_pairs={{1,0},{2,1},{3,2},{4,3},{5,4},{6,5},{7,6},{8,7},{9,8},{10,9},{11,1... | collective-permute-start | bytes 294920 | tf_op jit(solution)/shard_map/ppermute | solution.py:21
  27.2 7.0 %copy-start.7 = (s32[8,256]{1,0:T(8,128)S(1)}, s32[8,256]{1,0:T(8,128)}, u32[]{:S(2)}) copy-start(s32[8,256]{1,0:T(8,128)} %region_ref.7) | copy-start | bytes 24580
